TPU v7x, 128 devices: a whole 4x4x4 slice. The times are simulated.
128 devices in a mesh: dp: 1, x: 128 (over z, y, x, core).
Axes of the slice: x: 4, y: 4, z: 4, core: 2. Of those that a mesh axis runs over, the one named last changes fastest.
Arguments:
- c_raw: bfloat16 [512, 1024, 512], P('dp', 'x')
- k_raw: bfloat16 [512, 1024, 64], P('dp', 'x')
- norm_gain: bfloat16 [512], replicated
- rope_cos: float32 [1024, 32], P('x')
- rope_sin: float32 [1024, 32], P('x')
- seq_lens: int32 [512], P('dp')
- q_lat: bfloat16 [512, 16, 512], P(('dp', 'x'))
- q_rope: bfloat16 [512, 16, 64], P(('dp', 'x'))
Outputs:
- output 1: bfloat16 [512, 1024, 512], P(('dp', 'x'))
- output 2: bfloat16 [512, 1024, 64], P(('dp', 'x'))
- output 3: bfloat16 [512, 16, 512], P(('dp', 'x'))
All inputs are finite; a program needn't handle non-finite values.
Results may differ from a plain program's by a relative error of at most 0.00589776.
Values are sent between devices in bfloat16 or wider.
A program may use at most 1 GiB of HBM per device.

v0:
```python
import jax
import jax.numpy as jnp
from jax import lax
from jax.sharding import PartitionSpec as P

NORM_EPS = 1e-6


def normed_rope(c_raw, k_raw, norm_gain, rope_cos, rope_sin, valid):
    lat_f32 = c_raw.astype(jnp.float32)
    inv_rms = lax.rsqrt(jnp.mean(lat_f32 * lat_f32, axis=-1, keepdims=True) + NORM_EPS)
    c_norm = jnp.where(valid[..., None], lat_f32 * inv_rms * norm_gain.astype(jnp.float32), 0.0)
    half_dim = k_raw.shape[-1] // 2
    key_f32 = k_raw.astype(jnp.float32)
    key_lo = key_f32[..., :half_dim]
    key_hi = key_f32[..., half_dim:]
    rotated = jnp.concatenate([key_lo * rope_cos - key_hi * rope_sin, key_hi * rope_cos + key_lo * rope_sin], axis=-1)
    k_rope = jnp.where(valid[..., None], rotated, 0.0)
    return c_norm.astype(jnp.bfloat16), k_rope.astype(jnp.bfloat16)


def latent_attention(q_lat, q_rope, c_cache, kr_cache, valid):
    attn_scale = (q_lat.shape[-1] + q_rope.shape[-1]) ** -0.5
    scores = jnp.einsum("rhk,rsk->rhs", q_lat, c_cache, preferred_element_type=jnp.float32)
    scores = scores + jnp.einsum("rhe,rse->rhs", q_rope, kr_cache, preferred_element_type=jnp.float32)
    scores = jnp.where(valid[:, None, :], scores * attn_scale, -1e30)
    weights = jnp.exp(scores - jnp.max(scores, axis=-1, keepdims=True))
    weight_sum = jnp.sum(weights, axis=-1)
    weighted = jnp.einsum("rhs,rsk->rhk", weights.astype(jnp.bfloat16), c_cache, preferred_element_type=jnp.float32)
    return (weighted / weight_sum[..., None]).astype(jnp.bfloat16)


def solution(mesh):
    seq_spec = P("dp", "x", None)
    req_spec = P(("dp", "x"), None, None)

    def local_step(c_raw, k_raw, norm_gain, rope_cos, rope_sin, seq_lens, q_lat, q_rope):
        dev_index = lax.axis_index("x")
        seq_local = c_raw.shape[1]
        req_local = q_lat.shape[0]
        positions = dev_index * seq_local + jnp.arange(seq_local)
        valid = positions[None, :] < seq_lens[:, None]
        c_norm, k_rope = normed_rope(c_raw, k_raw, norm_gain, rope_cos, rope_sin, valid)
        c_cache = lax.all_to_all(c_norm, "x", 0, 1, tiled=True)
        kr_cache = lax.all_to_all(k_rope, "x", 0, 1, tiled=True)
        own_lens = lax.dynamic_slice_in_dim(seq_lens, dev_index * req_local, req_local)
        own_valid = jnp.arange(c_cache.shape[1])[None, :] < own_lens[:, None]
        o_lat = latent_attention(q_lat, q_rope, c_cache, kr_cache, own_valid)
        return c_cache, kr_cache, o_lat

    return jax.shard_map(local_step, mesh=mesh, in_specs=(seq_spec, seq_spec, P(None), P("x", None), P("x", None), P("dp"), req_spec, req_spec), out_specs=(req_spec, req_spec, req_spec), check_vma=False)
```

profile of v0, /device:TPU:1, one launch (start us, length us, event | category | flops | bytes accessed | tf_op | source)
XLA Modules:
  0.0 102.4 jit_solution(13679598021069892681)
XLA Ops:
  0.7 1.9 %copy.34 = bf16[512,8,64]{2,1,0:T(8,128)(2,1)S(1)} copy(bf16[512,8,64]{0,2,1:T(8,128)(2,1)} %param.9) | data formatting | bytes 1048576 | tf_op args[1]
  2.6 0.1 convert_element_type.24
  2.7 0.1 broadcast_compare_fusion
  2.9 0.7 multiply_subtract_fusion
  3.6 1.7 %fusion.4 = bf16[512,8,64]{2,1,0:T(8,128)(2,1)S(1)} fusion(bf16[512,8,32]{2,1,0:T(8,128)(2,1)S(1)} %get-tuple-element.16, bf16[512,8,32]{2,1,0:T(8,128)(2,1)S(1)} %get-tuple-element.15, pred[512,8]{1,0:T(8,128)(4,1)S(1)} %broadcast_compare_fusion), kind=kLoop, calls=%fused_computation.8 | loop fusion | flops 1310720 | bytes 1052672 | tf_op jit(solution)/shard_map/convert_element_type | solution.py:19
  5.3 1.4 %reshape.68 = bf16[128,2,1024]{2,1,0:T(2,128)(2,1)} reshape(bf16[512,8,64]{2,1,0:T(8,128)(2,1)S(1)} %fusion.4) | data formatting | bytes 1048576
  6.7 11.5 %all-to-all-start.1 = ((bf16[128,2,1024]{2,1,0:T(2,128)(2,1)}), bf16[128,2,1024]{2,1,0:T(2,128)(2,1)S(1)}, u32[]{:S(2)}, u32[]{:S(2)}) async-start(bf16[128,2,1024]{2,1,0:T(2,128)(2,1)} %reshape.68), calls=%async_computation.1 | async-start | bytes 1048576 | tf_op jit(solution)/shard_map/all_to_all | solution.py:45
  18.2 3.1 %fusion = f32[512,8]{1,0:T(8,128)S(1)} fusion(bf16[512,8,512]{2,1,0:T(8,128)(2,1)} %param.8), kind=kLoop, calls=%fused_computation.2 | loop fusion | flops 6287360 | bytes 4210688 | tf_op jit(solution)/shard_map/reduce_sum | solution.py:11
  21.3 0.1 copy.31
  21.4 0.1 copy.32
  21.5 6.2 %fusion.3 = bf16[512,8,512]{2,1,0:T(8,128)(2,1)} fusion(bf16[512,8,512]{2,1,0:T(8,128)(2,1)} %param.8, f32[512]{0:T(512)S(1)} %convert_element_type.22, f32[512,8]{1,0:T(8,128)S(1)} %copy.32, pred[512,8]{1,0:T(8,128)(4,1)S(1)} %broadcast_compare_fusion), kind=kLoop, calls=%fused_computation.5 | loop fusion | flops 10485760 | bytes 8411136 | tf_op jit(solution)/shard_map/convert_element_type | solution.py:19
  27.7 3.8 %all-to-all-done.1 = bf16[128,2,1024]{2,1,0:T(2,128)(2,1)S(1)} async-done(((bf16[128,2,1024]{2,1,0:T(2,128)(2,1)}), bf16[128,2,1024]{2,1,0:T(2,128)(2,1)S(1)}, u32[]{:S(2)}, u32[]{:S(2)}) %all-to-all-start.1) | async-done | bytes 524320 | tf_op jit(solution)/shard_map/all_to_all | solution.py:45
  31.6 6.4 %all-to-all-start = ((bf16[512,8,512]{2,1,0:T(8,128)(2,1)}), bf16[512,8,512]{2,1,0:T(8,128)(2,1)}, u32[]{:S(2)}, u32[]{:S(2)}) async-start(bf16[512,8,512]{2,1,0:T(8,128)(2,1)} %fusion.3), calls=%async_computation | async-start | bytes 8388608 | tf_op jit(solution)/shard_map/all_to_all | solution.py:44
  38.0 0.1 dynamic_slice.3
  38.0 0.1 iota_compare_fusion
  38.1 0.6 reshape.69
  38.7 0.2 copy_bitcast_fusion.1
  38.9 1.1 %copy.37 = bf16[4,1024,64]{1,2,0:T(8,128)(2,1)} copy(bf16[4,1024,64]{2,1,0:T(8,128)(2,1)S(1)} %copy_bitcast_fusion.1) | data formatting | bytes 1048576
  40.0 56.5 %all-to-all-done = bf16[512,8,512]{2,1,0:T(8,128)(2,1)} async-done(((bf16[512,8,512]{2,1,0:T(8,128)(2,1)}), bf16[512,8,512]{2,1,0:T(8,128)(2,1)}, u32[]{:S(2)}, u32[]{:S(2)}) %all-to-all-start) | async-done | bytes 4194336 | tf_op jit(solution)/shard_map/all_to_all | solution.py:44
  96.6 2.6 %copy.44 = bf16[128,4,8,512]{3,2,0,1:T(8,128)(2,1)S(1)} copy(bf16[128,4,8,512]{3,2,1,0:T(8,128)(2,1)} %bitcast) | data formatting | bytes 8388608 | tf_op jit(solution)/shard_map/all_to_all | solution.py:44
  99.2 1.2 %fusion.14 = f32[4,1024,16]{1,2,0:T(8,128)S(1)} fusion(bf16[4,1024,512]{2,1,0:T(8,128)(2,1)S(1)} %bitcast.22, bf16[4,16,512]{2,1,0:T(8,128)(2,1)S(1)} %copy-done), kind=kOutput, calls=%fused_computation.27 | convolution fusion | flops 67108864 | bytes 4521984 | tf_op jit(solution)/shard_map/rhk,rsk->rhs/dot_general | solution.py:24
  100.4 0.5 fusion.13
  100.9 0.2 fusion.9
  101.1 1.3 %fusion.8 = bf16[4,16,512]{2,1,0:T(8,128)(2,1)} fusion(bf16[4,1024,512]{2,1,0:T(8,128)(2,1)S(1)} %bitcast.23, f32[4,16,1024]{2,1,0:T(8,128)S(1)} %get-tuple-element.18, f32[4,16]{1,0:T(4,128)S(1)} %get-tuple-element.17, f32[4,16]{1,0:T(4,128)S(1)} %fusion.9), kind=kOutput, calls=%fused_computation.16 | convolution fusion | flops 67305472 | bytes 4522496 | tf_op jit(solution)/shard_map/rhs,rsk->rhk/dot_general | solution.py:29
  (17 shorter events, 0.1 us)
Async XLA Ops:
  0.6 98.6 %copy-start = (bf16[4,16,512]{2,1,0:T(8,128)(2,1)S(1)}, bf16[4,16,512]{2,1,0:T(8,128)(2,1)}, u32[]{:S(2)}) copy-start(bf16[4,16,512]{2,1,0:T(8,128)(2,1)} %param.14) | copy-start | bytes 196612
  0.6 2.1 %copy-start.4 = (s32[512]{0:T(512)S(1)}, s32[512]{0:T(512)}, u32[]{:S(2)}) copy-start(s32[512]{0:T(512)} %param.13) | copy-start | bytes 6148
  0.7 2.2 %copy-start.2 = (f32[8,32]{1,0:T(8,128)S(1)}, f32[8,32]{1,0:T(8,128)}, u32[]{:S(2)}) copy-start(f32[8,32]{1,0:T(8,128)} %param.12) | copy-start | bytes 3076
  0.7 2.2 %copy-start.3 = (f32[8,32]{1,0:T(8,128)S(1)}, f32[8,32]{1,0:T(8,128)}, u32[]{:S(2)}) copy-start(f32[8,32]{1,0:T(8,128)} %param.11) | copy-start | bytes 3076
  3.6 14.6 %copy-start.5 = (bf16[512]{0:T(512)(128)(2,1)S(1)}, bf16[512]{0:T(512)(128)(2,1)}, u32[]{:S(2)}) copy-start(bf16[512]{0:T(512)(128)(2,1)} %param.10) | copy-start | bytes 3076
  6.7 24.9 %all-to-all-start.1 = ((bf16[128,2,1024]{2,1,0:T(2,128)(2,1)}), bf16[128,2,1024]{2,1,0:T(2,128)(2,1)S(1)}, u32[]{:S(2)}, u32[]{:S(2)}) async-start(bf16[128,2,1024]{2,1,0:T(2,128)(2,1)} %reshape.68), calls=%async_computation.1 | async-start | bytes 1048576 | tf_op jit(solution)/shard_map/all_to_all | solution.py:45
  31.6 65.0 %all-to-all-start = ((bf16[512,8,512]{2,1,0:T(8,128)(2,1)}), bf16[512,8,512]{2,1,0:T(8,128)(2,1)}, u32[]{:S(2)}, u32[]{:S(2)}) async-start(bf16[512,8,512]{2,1,0:T(8,128)(2,1)} %fusion.3), calls=%async_computation | async-start | bytes 8388608 | tf_op jit(solution)/shard_map/all_to_all | solution.py:44
  99.2 3.3 %copy-start.1 = (bf16[128,4,8,512]{3,2,0,1:T(8,128)(2,1)}, bf16[128,4,8,512]{3,2,0,1:T(8,128)(2,1)S(1)}, u32[]{:S(2)}) copy-start(bf16[128,4,8,512]{3,2,0,1:T(8,128)(2,1)S(1)} %copy.44) | copy-start | bytes 12582916
  99.2 1.2 %copy-start.6 = (bf16[4,16,64]{2,1,0:T(8,128)(2,1)S(1)}, bf16[4,16,64]{2,1,0:T(8,128)(2,1)}, u32[]{:S(2)}) copy-start(bf16[4,16,64]{2,1,0:T(8,128)(2,1)} %param.15) | copy-start | bytes 24580
where the time goes:
time: 104 us; the launch traced here: 102 us
  waiting for transfers between devices  60.4 us (58%)
  starting transfers between devices  17.9 us (17%)
  other arithmetic  12.2 us (12%)
  local copies, waits for them, and re-layouts  8.06 us (8%)
  matrix products  3.02 us (3%)
    all_to_all x1, waiting for transfers between devices, local_step(): c_cache = lax.all_to_all(c_norm, 'x', 0, 1, tiled=True)  56.5 us
    all_to_all x1, starting transfers between devices, local_step(): kr_cache = lax.all_to_all(k_rope, 'x', 0, 1, tiled=True)  11.5 us
    convert_element_type x2, other arithmetic, normed_rope(): return (c_norm.astype(jnp.bfloat16), k_rope.astype(jnp.bfloat16))  7.85 us
    all_to_all x1, starting transfers between devices, local_step(): c_cache = lax.all_to_all(c_norm, 'x', 0, 1, tiled=True)  6.37 us
    unnamed x18, local copies, waits for them, and re-layouts  5.01 us
    all_to_all x1, waiting for transfers between devices, local_step(): kr_cache = lax.all_to_all(k_rope, 'x', 0, 1, tiled=True)  3.85 us
    reduce_sum x1, other arithmetic, normed_rope(): jnp.mean(lat_f32 * lat_f32, axis=-1, keepdims=True) + NORM_EPS  3.09 us
    all_to_all x1, local copies, waits for them, and re-layouts, local_step(): c_cache = lax.all_to_all(c_norm, 'x', 0, 1, tiled=True)  2.58 us
  transfers between devices with their start and end apart: 2, of which 2 were waited for; matrix products, arithmetic and copies ran while one was open for 11% of the time, Pallas kernels for 0%

commit v1 on v0

v1 whole, which is shorter than its diff:
```python
import jax
import jax.numpy as jnp
from jax import lax
from jax.experimental import pallas as pl
from jax.experimental.pallas import tpu as pltpu
from jax.sharding import PartitionSpec as P

NORM_EPS = 1e-6
ORDERS = ((0, 1, 2), (1, 2, 0), (2, 0, 1))
FULL = (4, 4, 4, 2, 8, 768)
COPIES = 66


def exchange_kernel(c_ref, k_ref, out0, out1, out2, *scratch):
    outs = (out0, out1, out2)
    src, mid1, mid2 = scratch[0:3], scratch[3:6], scratch[6:9]
    hop1, hop2, hop3 = scratch[9:15], scratch[15:21], scratch[21:27]
    load_sem, send_sem, recv_sem = scratch[27:30]

    me = lax.axis_index("x")
    core = me % 2
    cores = (core, 1 - core)
    place = (me // 32, (me // 8) % 4, (me // 2) % 4)

    def device(dim, delta, to_core=None):
        pos = list(place)
        pos[dim] = (pos[dim] + delta + 4) % 4
        last = core if to_core is None else to_core
        return ((pos[0] * 4 + pos[1]) * 4 + pos[2]) * 2 + last

    def at(dim, delta):
        return (place[dim] + delta + 4) % 4

    def view(ref, sel):
        return ref.at[tuple(pl.ds(*sel[d]) if d in sel else slice(None) for d in range(6))]

    loads = []
    n_load = 0

    def load(a, b):
        nonlocal n_load
        copy = pltpu.make_async_copy(a, b, load_sem.at[n_load])
        n_load += 1
        copy.start()
        loads.append(copy)

    def c_view(sel, req, cols):
        return c_ref.at[tuple(pl.ds(*sel[d]) if d in sel else slice(None) for d in range(4)) + (req, slice(None), pl.ds(*cols))]

    extra = ((3, (0, 256)), (3, (256, 256)))
    for p in range(3):
        load(c_view({}, p, (0, 512)), view(src[p], {5: (0, 512)}))
        if p < 2:
            load(c_view({}, *extra[p]), view(src[p], {5: (512, 256)}))
        else:
            load(k_ref, view(src[p], {5: (512, 256)}))
    for p in range(3):
        a = ORDERS[p][0]
        own = {a: (place[a], 1)}
        load(c_view(own, p, (0, 512)), view(mid1[p], {**own, 5: (0, 512)}))
        if p < 2:
            load(c_view(own, *extra[p]), view(mid1[p], {**own, 5: (512, 256)}))
        else:
            load(view(k_ref, own), view(mid1[p], {**own, 5: (512, 256)}))

    barrier = pltpu.get_barrier_semaphore()
    for dim in range(3):
        for delta in (1, -1):
            for k in range(2):
                pl.semaphore_signal(barrier, inc=1, device_id={"x": device(dim, delta, k)}, device_id_type=pl.DeviceIdType.MESH)
    pl.semaphore_signal(barrier, inc=1, device_id={"x": me + 1 - 2 * core}, device_id_type=pl.DeviceIdType.MESH)
    pl.semaphore_wait(barrier, 13)

    copies = [{} for _ in range(3)]

    def send(p, key, a, b, to):
        n = len(copies[p])
        copy = pltpu.make_async_remote_copy(src_ref=a, dst_ref=b, send_sem=send_sem.at[p, n], recv_sem=recv_sem.at[p, n], device_id={"x": to}, device_id_type=pl.DeviceIdType.MESH)
        copies[p][key] = copy
        copy.start()

    def arrived(p, *keys):
        for key in keys:
            copies[p][key].wait_recv()

    SIGNS = (1, -1)

    def phase1(p):
        a, b, _ = ORDERS[p]
        for s, sign in enumerate(SIGNS):
            send(p, ("1far", s), view(src[p], {a: (at(a, 2), 1), b: (2 * s, 2)}), hop1[2 * p + s], device(a, sign))
        for s, sign in enumerate(SIGNS):
            send(p, ("1near", s), view(src[p], {a: (at(a, sign), 1)}), view(mid1[p], {a: (place[a], 1)}), device(a, sign))

    def forward1(p):
        a, b, _ = ORDERS[p]
        for s, sign in enumerate(SIGNS):
            arrived(p, ("1far", s))
            send(p, ("1fwd", s), hop1[2 * p + s], view(mid1[p], {a: (at(a, -sign), 1), b: (2 * s, 2)}), device(a, sign))

    def phase2(p, off):
        a, b, c = ORDERS[p]
        sa = {a: (at(a, off), 1)}
        hop_sa = {a: (off % 4, 1)}
        for s, sign in enumerate(SIGNS):
            send(p, ("2far", off, s), view(mid1[p], {**sa, b: (at(b, 2), 1), c: (2 * s, 2)}), view(hop2[2 * p + s], hop_sa), device(b, sign))
        for s, sign in enumerate(SIGNS):
            send(p, ("2near", off, s), view(mid1[p], {**sa, b: (at(b, sign), 1)}), view(mid2[p], {**sa, b: (place[b], 1)}), device(b, sign))

    def forward2(p, off):
        a, b, c = ORDERS[p]
        sa = {a: (at(a, off), 1)}
        hop_sa = {a: (off % 4, 1)}
        for s, sign in enumerate(SIGNS):
            arrived(p, ("2far", off, s))
            send(p, ("2fwd", off, s), view(hop2[2 * p + s], hop_sa), view(mid2[p], {**sa, b: (at(b, -sign), 1), c: (2 * s, 2)}), device(b, sign))

    def phase3(p, off):
        a, b, c = ORDERS[p]
        sb = {b: (at(b, off), 1)}
        hop_sb = {b: (off % 4, 1)}
        held = mid1[p] if off == 0 else mid2[p]
        mine = {**sb, c: (place[c], 1), 3: (core, 1)}
        for s, sign in enumerate(SIGNS):
            send(p, ("3far", off, s), view(held, {**sb, c: (at(c, 2), 1), 3: (cores[s], 1)}), view(hop3[2 * p + s], hop_sb), device(c, sign))
        for s, sign in enumerate(SIGNS):
            for k in range(2):
                send(p, ("3near", off, s, k), view(held, {**sb, c: (at(c, sign), 1), 3: (cores[k], 1)}), view(outs[p], mine), device(c, sign, cores[k]))
        send(p, ("3core", off), view(held, {**sb, c: (place[c], 1), 3: (cores[1], 1)}), view(outs[p], mine), me + 1 - 2 * core)
        index = tuple(pl.ds(*mine[d]) if d in mine else slice(None) for d in range(6))
        outs[p][index] = held[index]

    def forward3(p, off):
        a, b, c = ORDERS[p]
        sb = {b: (at(b, off), 1)}
        hop_sb = {b: (off % 4, 1)}
        for s, sign in enumerate(SIGNS):
            arrived(p, ("3far", off, s))
            send(p, ("3fwd", off, s), view(hop3[2 * p + s], hop_sb), view(outs[p], {**sb, c: (at(c, -sign), 1), 3: (core, 1)}), device(c, sign, cores[s]))

    for copy in loads:
        copy.wait()
    for p in range(3):
        phase1(p)
    for p in range(3):
        forward1(p)
        phase2(p, 0)
    for p in range(3):
        arrived(p, ("1near", 0), ("1near", 1))
        phase2(p, -1)
        phase2(p, 1)
    for p in range(3):
        forward2(p, 0)
    for p in range(3):
        arrived(p, ("1fwd", 0), ("1fwd", 1))
        phase2(p, 2)
    for p in range(3):
        forward2(p, -1)
        forward2(p, 1)
    for p in range(3):
        forward2(p, 2)
        phase3(p, 0)
    for p in range(3):
        for off in (0, -1, 1, 2):
            arrived(p, ("2near", off, 0), ("2near", off, 1))
        phase3(p, -1)
        phase3(p, 1)
    for p in range(3):
        forward3(p, 0)
    for p in range(3):
        for off in (0, -1, 1, 2):
            arrived(p, ("2fwd", off, 0), ("2fwd", off, 1))
        phase3(p, 2)
    for p in range(3):
        forward3(p, -1)
        forward3(p, 1)
    for p in range(3):
        forward3(p, 2)
    for p in range(3):
        for key in copies[p]:
            if key[0] in ("3near", "3core", "3fwd"):
                arrived(p, key)
    for p in range(3):
        for copy in copies[p].values():
            copy.wait_send()


def exchange(c_raw, keys):
    part = pltpu.VMEM(FULL, jnp.bfloat16)

    def shaped(sizes):
        return pltpu.VMEM(tuple(sizes.get(d, FULL[d]) for d in range(6)), jnp.bfloat16)

    hop1 = [shaped({o[0]: 1, o[1]: 2}) for o in ORDERS for _ in range(2)]
    hop2 = [shaped({o[1]: 1, o[2]: 2}) for o in ORDERS for _ in range(2)]
    hop3 = [shaped({o[2]: 1, 3: 1}) for o in ORDERS for _ in range(2)]
    return pl.pallas_call(
        exchange_kernel,
        out_shape=[jax.ShapeDtypeStruct(FULL, jnp.bfloat16)] * 3,
        in_specs=[pl.BlockSpec(memory_space=pl.ANY)] * 2,
        out_specs=[pl.BlockSpec(memory_space=pltpu.VMEM)] * 3,
        scratch_shapes=[part] * 9 + hop1 + hop2 + hop3 + [pltpu.SemaphoreType.DMA((12,)), pltpu.SemaphoreType.DMA((3, COPIES)), pltpu.SemaphoreType.DMA((3, COPIES))],
        compiler_params=pltpu.CompilerParams(collective_id=0, has_side_effects=True, vmem_limit_bytes=60 * 1024 * 1024),
        name="exchange",
    )(c_raw, keys)


def roped_keys(k_raw, rope_cos, rope_sin):
    half_dim = k_raw.shape[-1] // 2
    key_f32 = k_raw.astype(jnp.float32)
    key_lo = key_f32[..., :half_dim]
    key_hi = key_f32[..., half_dim:]
    return jnp.concatenate([key_lo * rope_cos - key_hi * rope_sin, key_hi * rope_cos + key_lo * rope_sin], axis=-1).astype(jnp.bfloat16)


def normed(c_raw, norm_gain, valid):
    lat_f32 = c_raw.astype(jnp.float32)
    inv_rms = lax.rsqrt(jnp.mean(lat_f32 * lat_f32, axis=-1, keepdims=True) + NORM_EPS)
    return jnp.where(valid[..., None], lat_f32 * inv_rms * norm_gain.astype(jnp.float32), 0.0).astype(jnp.bfloat16)


def latent_attention(q_lat, q_rope, c_cache, kr_cache, valid):
    attn_scale = (q_lat.shape[-1] + q_rope.shape[-1]) ** -0.5
    scores = jnp.einsum("rhk,rsk->rhs", q_lat, c_cache, preferred_element_type=jnp.float32)
    scores = scores + jnp.einsum("rhe,rse->rhs", q_rope, kr_cache, preferred_element_type=jnp.float32)
    scores = jnp.where(valid[:, None, :], scores * attn_scale, -1e30)
    weights = jnp.exp(scores - jnp.max(scores, axis=-1, keepdims=True))
    weight_sum = jnp.sum(weights, axis=-1)
    weighted = jnp.einsum("rhs,rsk->rhk", weights.astype(jnp.bfloat16), c_cache, preferred_element_type=jnp.float32)
    return (weighted / weight_sum[..., None]).astype(jnp.bfloat16)


def solution(mesh):
    seq_spec = P("dp", "x", None)
    req_spec = P(("dp", "x"), None, None)

    def local_step(c_raw, k_raw, norm_gain, rope_cos, rope_sin, seq_lens, q_lat, q_rope):
        dev_index = lax.axis_index("x")
        keys = roped_keys(k_raw, rope_cos, rope_sin)
        keys = keys.reshape(128, 4, 8, 64).transpose(0, 2, 1, 3).reshape(4, 4, 4, 2, 8, 256)
        got = exchange(c_raw.reshape(4, 4, 4, 2, 4, 8, 512), keys)
        got = [part.reshape(1024, 768) for part in got]
        c_own = jnp.stack([got[0][:, :512], got[1][:, :512], got[2][:, :512], jnp.concatenate([got[0][:, 512:], got[1][:, 512:]], axis=1)])
        kr_own = got[2][:, 512:].reshape(1024, 4, 64).transpose(1, 0, 2)
        own_lens = lax.dynamic_slice_in_dim(seq_lens, dev_index * 4, 4)
        valid = jnp.arange(1024)[None, :] < own_lens[:, None]
        c_cache = normed(c_own, norm_gain, valid)
        kr_cache = jnp.where(valid[..., None], kr_own, jnp.bfloat16(0))
        o_lat = latent_attention(q_lat, q_rope, c_cache, kr_cache, valid)
        return c_cache, kr_cache, o_lat

    return jax.shard_map(local_step, mesh=mesh, in_specs=(seq_spec, seq_spec, P(None), P("x", None), P("x", None), P("dp"), req_spec, req_spec), out_specs=(req_spec, req_spec, req_spec), check_vma=False)
```

time: 104 us -> 89.9 us (0.86); the launches traced: 102 us -> 89.5 us
  Pallas kernels: 0 us -> 65.3 us
  waiting for transfers between devices: 60.4 us -> 0 us
  starting transfers between devices: 17.9 us -> 0 us
  local copies, waits for them, and re-layouts: 8.06 us -> 10.6 us
  other arithmetic: 12.2 us -> 10.1 us
    pallas_call x0 -> x1, Pallas kernels: none -> 65.3 us  [exchange(): pl.pallas_call(exchange_kernel, out_shape=[jax.ShapeDtypeStruct(FULL, jnp...]
    all_to_all x2 -> x0, waiting for transfers between devices: 60.4 us -> none  [the longest x1 56.5 us: local_step(): c_cache = lax.all_to_all(c_norm, 'x', 0, 1, tiled=True)]
    all_to_all x2 -> x0, starting transfers between devices: 17.9 us -> none  [the longest x1 11.5 us: local_step(): kr_cache = lax.all_to_all(k_rope, 'x', 0, 1, tiled=True)]
    slice x0 -> x4, local copies, waits for them, and re-layouts: none -> 5.17 us  [the longest x2 2.86 us: local_step(): kr_own = got[2][:, 512:].reshape(1024, 4, 64).transpose(1, 0, 2)]
    unnamed x18 -> x14, local copies, waits for them, and re-layouts: 5.01 us -> 0.04 us
    convert_element_type x4 -> x3, other arithmetic: 7.99 us -> 3.51 us  [the longest x1 1.67 us: normed(): jnp.where(valid[..., None], lat_f32 * inv_rms * norm_gain.astype(jnp.floa...]
    all_to_all x2 -> x0, local copies, waits for them, and re-layouts: 2.76 us -> none  [the longest x1 2.58 us: local_step(): c_cache = lax.all_to_all(c_norm, 'x', 0, 1, tiled=True)]
    another operation x0 -> x3, local copies, waits for them, and re-layouts: none -> 2.68 us
  transfers between devices with their start and end apart: 2 -> 0, of which waited for: 2 -> 0; matrix products, arithmetic and copies ran while one was open for 11% -> 0% of each run, Pallas kernels for 0% -> 0%
where the time goes in v1:
time: 89.9 us; the launch traced here: 89.5 us
  Pallas kernels  65.3 us (73%)
  local copies, waits for them, and re-layouts  10.6 us (12%)
  other arithmetic  10.1 us (11%)
  matrix products  2.82 us (3%)
    pallas_call x1, Pallas kernels, exchange(): pl.pallas_call(exchange_kernel, out_shape=[jax.ShapeDtypeStruct(FULL, jnp...  65.3 us
    slice x2, local copies, waits for them, and re-layouts, local_step(): kr_own = got[2][:, 512:].reshape(1024, 4, 64).transpose(1, 0, 2)  2.86 us
    reduce_sum x1, other arithmetic, normed(): jnp.mean(lat_f32 * lat_f32, axis=-1, keepdims=True) + NORM_EPS  2.22 us

profile of v1, /device:TPU:1, one launch (start us, length us, event | category | flops | bytes accessed | tf_op | source)
XLA Modules:
  0.0 89.5 jit_solution(12410580205579900517)
XLA Ops:
  0.6 0.8 dynamic_slice.3
  1.4 0.7 convert_element_type.22
  2.1 0.1 iota_compare_fusion
  2.2 1.2 %convert_element_type.20 = f32[512,8,64]{0,2,1:T(8,128)S(1)} convert(bf16[512,8,64]{0,2,1:T(8,128)(2,1)} %param.9) | non-fusion elementwise | flops 262144 | bytes 1572864 | tf_op jit(solution)/shard_map/convert_element_type | solution.py:210
  3.4 0.9 %subtract_convert_fusion = (bf16[512,8,32]{0,2,1:T(8,128)(2,1)S(1)}, bf16[512,8,32]{0,2,1:T(8,128)(2,1)S(1)}) fusion(f32[512,8,64]{0,2,1:T(8,128)S(1)} %convert_element_type.20, f32[8,32]{1,0:T(8,128)} %param.12, f32[8,32]{1,0:T(8,128)} %param.11), kind=kLoop, calls=%fused_computation.19 | loop fusion | flops 1048576 | bytes 1574912 | tf_op jit(solution)/shard_map/convert.3
  4.3 0.8 copy.14
  5.0 0.8 copy.15
  5.8 0.6 maximum_bitcast_fusion
  6.4 0.4 copy.16
  6.8 1.5 %reshape.79.k_ref = bf16[4,4,4,2,8,256]{5,4,3,2,1,0:T(8,128)(2,1)} reshape(bf16[128,8,4,64]{3,2,1,0:T(4,128)(2,1)S(1)} %copy.16) | data formatting | bytes 1048576 | tf_op jit(solution)/shard_map/reshape | solution.py:240
  8.3 65.3 %exchange.1 = (bf16[4,4,4,2,8,768]{5,4,3,2,1,0:T(8,128)(2,1)}, bf16[4,4,4,2,8,768]{5,4,3,2,1,0:T(8,128)(2,1)}, bf16[4,4,4,2,8,768]{5,4,3,2,1,0:T(8,128)(2,1)}) custom-call(bf16[4,4,4,2,4,8,512]{6,5,4,3,2,1,0:T(8,128)(2,1)} %bitcast.28, bf16[4,4,4,2,8,256]{5,4,3,2,1,0:T(8,128)(2,1)} %reshape.79.k_ref), custom_call_target="tpu_custom_call" | custom-call | tf_op jit(solution)/shard_map/exchange/pallas_call | solution.py:197
  73.6 1.2 %slice.38 = bf16[1024,256]{1,0:T(8,128)(2,1)S(1)} slice(bf16[1024,768]{1,0:T(8,128)(2,1)} %bitcast.30), slice={[0:1024], [512:768]} | slice | bytes 1048576 | tf_op jit(solution)/shard_map/slice | solution.py:243
  74.8 1.1 %slice.37 = bf16[1024,256]{1,0:T(8,128)(2,1)S(1)} slice(bf16[1024,768]{1,0:T(8,128)(2,1)} %bitcast.34), slice={[0:1024], [512:768]} | slice | bytes 1048576 | tf_op jit(solution)/shard_map/slice | solution.py:243
  75.9 1.4 %slice_bitcast_fusion.2 = (bf16[1,1024,512]{2,1,0:T(8,128)(2,1)S(1)}, bf16[1,1024,512]{2,1,0:T(8,128)(2,1)S(1)}) fusion(bf16[1024,768]{1,0:T(8,128)(2,1)} %bitcast.35, bf16[1024,256]{1,0:T(8,128)(2,1)S(1)} %slice.38, bf16[1024,256]{1,0:T(8,128)(2,1)S(1)} %slice.37), kind=kLoop, calls=%fused_computation.15 | loop fusion | flops 2097152 | bytes 4194304 | tf_op jit(solution)/shard_map/stack | solution.py:243
  77.3 0.8 slice.39
  78.2 1.1 %slice_bitcast_fusion = (bf16[1,1024,512]{2,1,0:T(8,128)(2,1)S(1)}, bf16[1,1024,512]{2,1,0:T(8,128)(2,1)}) fusion(bf16[1024,768]{1,0:T(8,128)(2,1)S(1)} %bitcast.33, bf16[1024,768]{1,0:T(8,128)(2,1)S(1)} %bitcast.31), kind=kLoop, calls=%fused_computation.13 | loop fusion | bytes 4194304 | tf_op jit(solution)/shard_map/stack | solution.py:243
  79.3 2.0 %copy.17 = bf16[1024,256]{0,1:T(8,128)(2,1)} copy(bf16[1024,256]{1,0:T(8,128)(2,1)} %slice.39) | data formatting | bytes 1048576 | tf_op jit(solution)/shard_map/slice | solution.py:244
  81.4 1.2 %broadcast_select_fusion = bf16[4,1024,64]{1,2,0:T(8,128)(2,1)S(1)} fusion(bf16[4,1024,64]{1,2,0:T(8,128)(2,1)} %bitcast.29, pred[4,1024]{1,0:T(4,128)(4,1)S(1)} %iota_compare_fusion), kind=kLoop, calls=%fused_computation.20 | loop fusion | flops 262144 | bytes 1052672 | tf_op jit(solution)/shard_map/jit(_where)/select_n | solution.py:248
  82.5 2.2 %fusion = f32[4,1024]{1,0:T(4,128)S(1)} fusion(bf16[1,1024,512]{2,1,0:T(8,128)(2,1)S(1)} %get-tuple-element.16, bf16[1,1024,512]{2,1,0:T(8,128)(2,1)S(1)} %get-tuple-element.13, bf16[1,1024,512]{2,1,0:T(8,128)(2,1)} %get-tuple-element.14, bf16[1,1024,512]{2,1,0:T(8,128)(2,1)S(1)} %get-tuple-element.15), kind=kLoop, calls=%fused_computation.2 | loop fusion | flops 12578816 | bytes 4210688 | tf_op jit(solution)/shard_map/reduce_sum | solution.py:218
  84.8 1.7 %fusion.3 = bf16[4,1024,512]{2,1,0:T(8,128)(2,1)S(1)} fusion(f32[512]{0:T(512)S(1)} %convert_element_type.22, f32[4,1024]{1,0:T(4,128)S(1)} %add_rsqrt_fusion, pred[4,1024]{1,0:T(4,128)(4,1)S(1)} %iota_compare_fusion, bf16[1,1024,512]{2,1,0:T(8,128)(2,1)S(1)} %get-tuple-element.16, bf16[1,1024,512]{2,1,0:T(8,128)(2,1)S(1)} %get-tuple-element.13, ...), kind=kLoop, calls=%fused_computation.5 | loop fusion | flops 16777216 | bytes 8411136 | tf_op jit(solution)/shard_map/convert_element_type | solution.py:219
  86.5 1.2 %fusion.13 = f32[4,1024,16]{1,2,0:T(8,128)S(1)} fusion(bf16[4,1024,512]{2,1,0:T(8,128)(2,1)S(1)} %fusion.3, bf16[4,16,512]{2,1,0:T(8,128)(2,1)S(1)} %copy-done), kind=kOutput, calls=%fused_computation.28 | convolution fusion | flops 67108864 | bytes 4521984 | tf_op jit(solution)/shard_map/rhk,rsk->rhs/dot_general | solution.py:224
  87.7 0.3 fusion.12
  88.0 0.2 fusion.8
  88.2 1.3 %fusion.7 = bf16[4,16,512]{2,1,0:T(8,128)(2,1)} fusion(bf16[4,1024,512]{2,1,0:T(8,128)(2,1)S(1)} %fusion.3, f32[4,16,1024]{2,1,0:T(8,128)S(1)} %get-tuple-element.12, f32[4,16]{1,0:T(4,128)S(1)} %get-tuple-element.11, f32[4,16]{1,0:T(4,128)S(1)} %fusion.8), kind=kOutput, calls=%fused_computation.12 | convolution fusion | flops 67305472 | bytes 4522496 | tf_op jit(solution)/shard_map/rhs,rsk->rhk/dot_general | solution.py:229
  (15 shorter events, 0.1 us)
Async XLA Ops:
  0.6 85.8 %copy-start = (bf16[4,16,512]{2,1,0:T(8,128)(2,1)S(1)}, bf16[4,16,512]{2,1,0:T(8,128)(2,1)}, u32[]{:S(2)}) copy-start(bf16[4,16,512]{2,1,0:T(8,128)(2,1)} %param.14) | copy-start | bytes 196612
  73.6 3.7 %copy-start.5 = (bf16[4,4,4,2,8,768]{5,4,3,2,1,0:T(8,128)(2,1)S(1)}, bf16[4,4,4,2,8,768]{5,4,3,2,1,0:T(8,128)(2,1)}, u32[]{:S(2)}) copy-start(bf16[4,4,4,2,8,768]{5,4,3,2,1,0:T(8,128)(2,1)} %get-tuple-element.8) | copy-start | bytes 4718596
  73.6 4.6 %copy-start.4 = (bf16[4,4,4,2,8,768]{5,4,3,2,1,0:T(8,128)(2,1)S(1)}, bf16[4,4,4,2,8,768]{5,4,3,2,1,0:T(8,128)(2,1)}, u32[]{:S(2)}) copy-start(bf16[4,4,4,2,8,768]{5,4,3,2,1,0:T(8,128)(2,1)} %get-tuple-element.7) | copy-start | bytes 4718596
  81.4 3.4 %copy-start.2 = (bf16[1,1024,512]{2,1,0:T(8,128)(2,1)S(1)}, bf16[1,1024,512]{2,1,0:T(8,128)(2,1)}, u32[]{:S(2)}) copy-start(bf16[1,1024,512]{2,1,0:T(8,128)(2,1)} %get-tuple-element.14) | copy-start | bytes 3145732
  82.5 5.2 %copy-start.3 = (bf16[4,1024,64]{1,2,0:T(8,128)(2,1)}, bf16[4,1024,64]{1,2,0:T(8,128)(2,1)S(1)}, u32[]{:S(2)}) copy-start(bf16[4,1024,64]{1,2,0:T(8,128)(2,1)S(1)} %broadcast_select_fusion) | copy-start | bytes 1572868
  86.5 3.1 %copy-start.1 = (bf16[4,1024,512]{2,1,0:T(8,128)(2,1)}, bf16[4,1024,512]{2,1,0:T(8,128)(2,1)S(1)}, u32[]{:S(2)}) copy-start(bf16[4,1024,512]{2,1,0:T(8,128)(2,1)S(1)} %fusion.3) | copy-start | bytes 12582916
  86.5 1.2 %copy-start.6 = (bf16[4,16,64]{2,1,0:T(8,128)(2,1)S(1)}, bf16[4,16,64]{2,1,0:T(8,128)(2,1)}, u32[]{:S(2)}) copy-start(bf16[4,16,64]{2,1,0:T(8,128)(2,1)} %param.15) | copy-start | bytes 24580

commit v2 on v0

v2 whole, which is shorter than its diff:
```python
import jax
import jax.numpy as jnp
from jax import lax
from jax.experimental import pallas as pl
from jax.experimental.pallas import tpu as pltpu
from jax.sharding import PartitionSpec as P

NORM_EPS = 1e-6
ATTN_SCALE = (512 + 64) ** -0.5
ORDERS = ((0, 1, 2), (1, 2, 0), (2, 0, 1))
FULL = (4, 4, 4, 2, 8, 768)
STRIDES = (256, 64, 16)
POSITIONS, LATENT, ROPE, HEADS, LANES = 1024, 512, 64, 16, 128
ROWS = 64
KEY_COLS = 256
C_COLS, K_COLS, ALL_COLS = (0, LATENT), (LATENT, KEY_COLS), (0, LATENT + KEY_COLS)
CORE, COL = 3, 5
PARTS = range(3)
PAIR = range(2)
REQUESTS = range(4)
REQ = 512
COPIES = 80
LOADS = 27
SIGNS = (1, -1)
OFFSETS = (0, -1, 1, 2)
NT = (((1,), (1,)), ((), ()))
F32, BF16 = jnp.float32, jnp.bfloat16


def exchange_kernel(c_ref, k_ref, cos_ref, sin_ref, gain_ref, len_ref, qlat_ref, qrope_ref, c_out, kr_out, score_out, len_out, scratch):
    src, mid1, mid2, got, hop1, hop2, hop3, small, sems = scratch
    k_buf, cos_buf, sin_buf, gain_buf, len_buf, qlat_buf, qrope_buf, q_rows, qk_rows = small
    load_sem, send_sem, recv_sem = sems

    me = lax.axis_index("x")
    core = me % 2
    other = me + 1 - 2 * core
    cores = (core, 1 - core)
    place = (me // 32, (me // 8) % 4, (me // 2) % 4)

    def device(dim, delta, to_core=None):
        pos = list(place)
        pos[dim] = (pos[dim] + delta + 4) % 4
        last = core if to_core is None else to_core
        return ((pos[0] * 4 + pos[1]) * 4 + pos[2]) * 2 + last

    def at(dim, delta):
        return (place[dim] + delta + 4) % 4

    def index(sel, dims=len(FULL)):
        return tuple(pl.ds(*sel[d]) if d in sel else slice(None) for d in range(dims))

    def one(i):
        return (i, 1)

    def halves(s):
        return (2 * s, 2)

    def view(ref, sel):
        return ref.at[index(sel)]

    barrier = pltpu.get_barrier_semaphore()
    for dim in PARTS:
        for delta in SIGNS:
            for k in PAIR:
                pl.semaphore_signal(barrier, inc=1, device_id={"x": device(dim, delta, k)}, device_id_type=pl.DeviceIdType.MESH)
    pl.semaphore_signal(barrier, inc=1, device_id={"x": other}, device_id_type=pl.DeviceIdType.MESH)

    loads = {}

    def load(key, a, b):
        copy = pltpu.make_async_copy(a, b, load_sem.at[len(loads)])
        loads[key] = copy
        copy.start()

    def loaded(*keys):
        for key in keys:
            loads[key].wait()

    def load_slab(p, off, into, key):
        a = ORDERS[p][0]
        sel = {a: one(at(a, off))}
        rows = index(sel, COL - 1)
        load((key, 0), c_ref.at[rows + (p, slice(None), pl.ds(*C_COLS))], view(into, {**sel, COL: C_COLS}))
        if p < 2:
            load((key, 1), c_ref.at[rows + (3, slice(None), pl.ds(KEY_COLS * p, KEY_COLS))], view(into, {**sel, COL: K_COLS}))

    load("k", k_ref, k_buf)
    load("cos", cos_ref, cos_buf)
    load("sin", sin_ref, sin_buf)
    for off in (2, 1, -1):
        for p in PARTS:
            load_slab(p, off, src[p], ("src", p, off))
    for p in PARTS:
        load_slab(p, 0, mid1[p], ("own", p))
    load("gain", gain_ref, gain_buf)
    load("len", len_ref, len_buf)
    load("qlat", qlat_ref, qlat_buf)
    load("qrope", qrope_ref, qrope_buf)

    copies = [{} for _ in PARTS]

    def send(p, key, a, b, to):
        n = len(copies[p])
        copy = pltpu.make_async_remote_copy(src_ref=a, dst_ref=b, send_sem=send_sem.at[p, n], recv_sem=recv_sem.at[p, n], device_id={"x": to}, device_id_type=pl.DeviceIdType.MESH)
        copies[p][key] = copy
        copy.start()

    def arrived(p, *keys):
        for key in keys:
            copies[p][key].wait_recv()

    def phase1(p, cols=ALL_COLS):
        a, b, _ = ORDERS[p]
        wide = {COL: cols}
        for s, sign in enumerate(SIGNS):
            send(p, ("1far", cols, s), view(src[p], {a: one(at(a, 2)), b: halves(s), **wide}), view(hop1[2 * p + s], wide), device(a, sign))
        for s, sign in enumerate(SIGNS):
            send(p, ("1near", cols, s), view(src[p], {a: one(at(a, sign)), **wide}), view(mid1[p], {a: one(place[a]), **wide}), device(a, sign))

    def forward1(p, cols=ALL_COLS):
        a, b, _ = ORDERS[p]
        wide = {COL: cols}
        for s, sign in enumerate(SIGNS):
            arrived(p, ("1far", cols, s))
            send(p, ("1fwd", cols, s), view(hop1[2 * p + s], wide), view(mid1[p], {a: one(at(a, -sign)), b: halves(s), **wide}), device(a, sign))

    def arrived1(p, kind):
        for key in list(copies[p]):
            if key[0] == kind:
                arrived(p, key)

    def phase2(p, off):
        a, b, c = ORDERS[p]
        sa = {a: one(at(a, off))}
        hop_sa = {a: one(off % 4)}
        for s, sign in enumerate(SIGNS):
            send(p, ("2far", off, s), view(mid1[p], {**sa, b: one(at(b, 2)), c: halves(s)}), view(hop2[2 * p + s], hop_sa), device(b, sign))
        for s, sign in enumerate(SIGNS):
            send(p, ("2near", off, s), view(mid1[p], {**sa, b: one(at(b, sign))}), view(mid2[p], {**sa, b: one(place[b])}), device(b, sign))

    def forward2(p, off):
        a, b, c = ORDERS[p]
        sa = {a: one(at(a, off))}
        hop_sa = {a: one(off % 4)}
        for s, sign in enumerate(SIGNS):
            arrived(p, ("2far", off, s))
            send(p, ("2fwd", off, s), view(hop2[2 * p + s], hop_sa), view(mid2[p], {**sa, b: one(at(b, -sign)), c: halves(s)}), device(b, sign))

    def phase3(p, off):
        a, b, c = ORDERS[p]
        sb = {b: one(at(b, off))}
        hop_sb = {b: one(off % 4)}
        held = mid1[p] if off == 0 else mid2[p]
        mine = {**sb, c: one(place[c]), CORE: one(core)}
        for s, sign in enumerate(SIGNS):
            send(p, ("3far", off, s), view(held, {**sb, c: one(at(c, 2)), CORE: one(cores[s])}), view(hop3[2 * p + s], hop_sb), device(c, sign))
        for s, sign in enumerate(SIGNS):
            for k in PAIR:
                send(p, ("3near", off, s, k), view(held, {**sb, c: one(at(c, sign)), CORE: one(cores[k])}), view(got[p], mine), device(c, sign, cores[k]))
        send(p, ("3core", off), view(held, {**sb, c: one(place[c]), CORE: one(cores[1])}), view(got[p], mine), other)
        got[p][index(mine)] = held[index(mine)]

    def forward3(p, off):
        a, b, c = ORDERS[p]
        sb = {b: one(at(b, off))}
        hop_sb = {b: one(off % 4)}
        for s, sign in enumerate(SIGNS):
            arrived(p, ("3far", off, s))
            send(p, ("3fwd", off, s), view(hop3[2 * p + s], hop_sb), view(got[p], {**sb, c: one(at(c, -sign)), CORE: one(core)}), device(c, sign, cores[s]))

    def length(j):
        return len_buf[4 * me + j]

    def keys():
        row = lax.broadcasted_iota(jnp.int32, (32, 32), 0)
        diag = row == lax.broadcasted_iota(jnp.int32, (32, 32), 1)
        roped = []
        for pos in range(8):
            cos = jnp.sum(jnp.where(diag, cos_buf[pos : pos + 1, :], 0.0), axis=1, keepdims=True)
            sin = jnp.sum(jnp.where(diag, sin_buf[pos : pos + 1, :], 0.0), axis=1, keepdims=True)
            lo = k_buf[pos, 0:32, :].astype(F32)
            hi = k_buf[pos, 32:64, :].astype(F32)
            roped.append(jnp.concatenate([lo * cos - hi * sin, hi * cos + lo * sin], axis=0).astype(BF16))
        out_row = lax.broadcasted_iota(jnp.int32, (256, 128), 0)
        lane = lax.broadcasted_iota(jnp.int32, (256, 128), 1)
        picks = [jnp.where((out_row % 8 == pos) & (out_row // 8 == lane // 4), 1.0, 0.0).astype(BF16) for pos in range(8)]
        pick = jnp.concatenate(picks, axis=1)
        request = lax.broadcasted_iota(jnp.int32, (64, 1024), 1) % 4
        for z in REQUESTS:
            cat = jnp.concatenate([r[:, 128 * z : 128 * (z + 1)] for r in roped], axis=1)
            masked = jnp.concatenate([jnp.where(request == j, cat, jnp.zeros_like(cat)) for j in REQUESTS], axis=0)
            laid = lax.dot_general(pick, masked, NT, preferred_element_type=F32)
            laid = laid.reshape(1, 4, 4, 2, 8, 256).astype(BF16)
            src[2][z : z + 1, :, :, :, :, 512:768] = laid
        own = {2: one(place[2]), COL: K_COLS}
        mid1[2][index(own)] = src[2][index(own)]

    def queries():
        q_rows[...] = jnp.zeros_like(q_rows)
        for j in REQUESTS:
            q_rows[j, HEADS * j : HEADS * (j + 1), :] = qlat_buf[j]
        zero = jnp.zeros((HEADS, ROPE), BF16)
        qk_rows[...] = jnp.zeros_like(qk_rows)
        for j in REQUESTS:
            qk_rows[HEADS * j : HEADS * (j + 1), :] = jnp.concatenate([qrope_buf[j] if i == j else zero for i in REQUESTS], axis=1)
        score_out[...] = jnp.zeros_like(score_out)
        lane = lax.broadcasted_iota(jnp.int32, (8, LANES), 1)
        lens = jnp.zeros((8, LANES), jnp.int32)
        for j in REQUESTS:
            lens = jnp.where(lane // HEADS == j, length(j), lens)
        len_out[...] = lens

    def row_positions(a, b, c, ib, ic):
        r = lax.broadcasted_iota(jnp.int32, (ROWS, 1), 0)
        return (r // 16) * STRIDES[a] + r % 16 + ib * STRIDES[b] + ic * STRIDES[c]

    def unit_shape(a, width):
        return tuple(4 if d == a else 1 for d in range(3)) + (2, 8, width)

    def finish_rows(j, raw, gain, positions, a, where):
        square = jnp.sum(raw * raw, axis=-1, keepdims=True) * (1.0 / 512)
        inv_rms = jnp.where(positions < length(j), lax.rsqrt(square + NORM_EPS), 0.0)
        c_norm = raw * inv_rms * gain
        c_out[(j,) + where] = c_norm.reshape(unit_shape(a, LATENT)).astype(BF16)
        part = lax.dot_general(c_norm.astype(BF16), q_rows[j], NT, preferred_element_type=F32)
        score_out[where] += part.reshape(unit_shape(a, LANES))

    def gain_row():
        return gain_buf[...].astype(F32).reshape(1, LATENT)

    def unit(p, ib, ic):
        a, b, c = ORDERS[p]
        where = index({b: one(ib), c: one(ic)})[:COL]
        gain = gain_row()
        raw = got[p][where + (pl.ds(*C_COLS),)].astype(F32).reshape(ROWS, LATENT)
        finish_rows(p, raw, gain, row_positions(a, b, c, ib, ic), a, where + (slice(None),))
        if p == 2:
            held = got[2][where + (pl.ds(*K_COLS),)].astype(F32).reshape(ROWS, KEY_COLS).astype(BF16)
            part = lax.dot_general(held, qk_rows[...], NT, preferred_element_type=F32)
            score_out[where + (slice(None),)] += part.reshape(unit_shape(a, LANES))

    def near_units(p, off):
        a, b, c = ORDERS[p]
        arrived(p, ("3core", off), *[("3near", off, s, k) for s in PAIR for k in PAIR])

        @pl.loop(0, 3)
        def _(i):
            unit(p, at(b, off), (place[c] + 3 + i) % 4)

    def far_unit(p, off):
        a, b, c = ORDERS[p]
        arrived(p, ("3fwd", off, 0), ("3fwd", off, 1))
        unit(p, at(b, off), at(c, 2))
        if p == 2:
            key_columns(at(b, off))

    def key_columns(z):
        row = lax.broadcasted_iota(jnp.int32, (KEY_COLS, KEY_COLS), 0)
        col = lax.broadcasted_iota(jnp.int32, (KEY_COLS, KEY_COLS), 1)
        eye = jnp.where(row == col, 1.0, 0.0).astype(BF16)
        held = got[2][pl.ds(z, 1), :, :, :, :, pl.ds(*K_COLS)].astype(F32).reshape(KEY_COLS, KEY_COLS).astype(BF16)
        turned = lax.dot_general(eye, held, NT, preferred_element_type=F32)
        for j in REQUESTS:
            valid = col[:ROPE] + z * KEY_COLS < length(j)
            kr_out[j, :, pl.ds(pl.multiple_of(z * KEY_COLS, KEY_COLS), KEY_COLS)] = jnp.where(valid, turned[ROPE * j : ROPE * (j + 1)], 0.0).astype(BF16)

    def last_request():
        @pl.loop(0, 16)
        def _(i):
            y, x = i // 4, i % 4
            where = index({1: one(y), 2: one(x)})[:COL]
            gain = gain_row()
            raw = [got[p][where + (pl.ds(*K_COLS),)].astype(F32).reshape(ROWS, KEY_COLS) for p in PAIR]
            finish_rows(3, jnp.concatenate(raw, axis=1), gain, row_positions(0, 1, 2, y, x), 0, where + (slice(None),))

    for off in (2, 1, -1):
        for p in PARTS:
            loaded((("src", p, off), 0))
            if p < 2:
                loaded((("src", p, off), 1))
    pl.semaphore_wait(barrier, 13)
    phase1(0)
    phase1(1)
    phase1(2, C_COLS)
    loaded("k", "cos", "sin")
    keys()
    loaded("gain", "len", "qlat", "qrope")
    queries()
    phase1(2, K_COLS)
    for p in PARTS:
        loaded((("own", p), 0))
        if p < 2:
            loaded((("own", p), 1))
    forward1(0)
    forward1(1)
    forward1(2, C_COLS)
    for p in PARTS:
        phase2(p, 0)
    forward1(2, K_COLS)
    for p in PARTS:
        arrived1(p, "1near")
        phase2(p, -1)
        phase2(p, 1)
    for p in PARTS:
        forward2(p, 0)
    for p in PARTS:
        arrived1(p, "1fwd")
        phase2(p, 2)
    for p in PARTS:
        forward2(p, -1)
        forward2(p, 1)
    for p in PARTS:
        forward2(p, 2)
        phase3(p, 0)
    for p in PARTS:
        for off in OFFSETS:
            arrived(p, ("2near", off, 0), ("2near", off, 1))
        phase3(p, -1)
    for p in PARTS:
        forward3(p, 0)
        phase3(p, 1)
    for p in PARTS:
        near_units(p, 0)
    for p in PARTS:
        for off in OFFSETS:
            arrived(p, ("2fwd", off, 0), ("2fwd", off, 1))
        forward3(p, -1)
        phase3(p, 2)
    for p in PARTS:
        near_units(p, -1)
        far_unit(p, 0)
    for p in PARTS:
        forward3(p, 1)
    for p in PARTS:
        near_units(p, 1)
        far_unit(p, -1)
    for p in PARTS:
        forward3(p, 2)
    for p in PARTS:
        near_units(p, 2)
        far_unit(p, 1)
    for p in PARTS:
        far_unit(p, 2)
    last_request()
    for p in PARTS:
        for copy in copies[p].values():
            copy.wait_send()


def exchange(c_raw, k_turned, rope_cos, rope_sin, gain, seq_lens, q_lat, q_rope):
    def shaped(sizes):
        return pltpu.VMEM(tuple(sizes.get(d, FULL[d]) for d in range(6)), BF16)

    hop1 = [shaped({o[0]: 1, o[1]: 2}) for o in ORDERS for _ in PAIR]
    hop2 = [shaped({o[1]: 1, o[2]: 2}) for o in ORDERS for _ in PAIR]
    hop3 = [shaped({o[2]: 1, 3: 1}) for o in ORDERS for _ in PAIR]
    small = [
        pltpu.VMEM((8, 64, 512), BF16),
        pltpu.VMEM((8, 32), F32),
        pltpu.VMEM((8, 32), F32),
        pltpu.VMEM((LATENT,), BF16),
        pltpu.SMEM((REQ,), jnp.int32),
        pltpu.VMEM((4, 16, 512), BF16),
        pltpu.VMEM((4, 16, 64), BF16),
        pltpu.VMEM((4, 128, 512), BF16),
        pltpu.VMEM((128, 256), BF16),
    ]
    sems = [pltpu.SemaphoreType.DMA((LOADS,)), pltpu.SemaphoreType.DMA((3, COPIES)), pltpu.SemaphoreType.DMA((3, COPIES))]
    return pl.pallas_call(
        exchange_kernel,
        out_shape=[
            pltpu.VMEM((4, 4, 4, 4, 2, 8, 512), BF16),
            pltpu.VMEM((4, 64, 1024), BF16),
            pltpu.VMEM((4, 4, 4, 2, 8, 128), F32),
            pltpu.VMEM((8, LANES), jnp.int32),
        ],
        in_specs=[pl.BlockSpec(memory_space=pltpu.HBM)] * 8,
        out_specs=[pl.BlockSpec(memory_space=pltpu.VMEM)] * 4,
        scratch_shapes=[[[shaped({})] * 3] * 4 + [hop1, hop2, hop3, small, sems]],
        compiler_params=pltpu.CompilerParams(collective_id=0, has_side_effects=True, vmem_limit_bytes=40 * 1024 * 1024),
        name="exchange",
    )(c_raw, k_turned, rope_cos, rope_sin, gain, seq_lens, q_lat, q_rope)


def attend_kernel(c_ref, kr_ref, score_ref, len_ref, c_out, kr_out, o_ref, sem):
    writes = [pltpu.make_async_copy(c_ref, c_out, sem.at[0]), pltpu.make_async_copy(kr_ref, kr_out, sem.at[1])]
    for write in writes:
        write.start()
    row = lax.broadcasted_iota(jnp.int32, (POSITIONS, LANES), 0)
    scores = jnp.where(row < len_ref[0:1, :], score_ref[...] * ATTN_SCALE, -1e30)
    weights = jnp.exp(scores - jnp.max(scores, axis=0, keepdims=True)).T
    weight_sum = jnp.sum(weights[: 4 * HEADS], axis=1, keepdims=True)
    rounded = weights[: 4 * HEADS].astype(BF16)
    for j in REQUESTS:
        mine = slice(HEADS * j, HEADS * (j + 1))
        weighted = jnp.dot(rounded[mine], c_ref[j], preferred_element_type=F32)
        o_ref[j] = (weighted / weight_sum[mine]).astype(BF16)
    for write in writes:
        write.wait()


def attend(c_cache, kr_turned, scores, lens):
    whole = pl.BlockSpec(memory_space=pltpu.VMEM)
    return pl.pallas_call(
        attend_kernel,
        out_shape=[
            jax.ShapeDtypeStruct(c_cache.shape, BF16),
            jax.ShapeDtypeStruct(kr_turned.shape, BF16),
            jax.ShapeDtypeStruct((4, HEADS, LATENT), BF16),
        ],
        in_specs=[whole] * 4,
        out_specs=[pl.BlockSpec(memory_space=pltpu.HBM)] * 2 + [whole],
        scratch_shapes=[pltpu.SemaphoreType.DMA((2,))],
        compiler_params=pltpu.CompilerParams(vmem_limit_bytes=24 * 1024 * 1024),
        name="attend",
    )(c_cache, kr_turned, scores, lens)


def solution(mesh):
    seq_spec = P("dp", "x", None)
    req_spec = P(("dp", "x"), None, None)

    def local_step(c_raw, k_raw, norm_gain, rope_cos, rope_sin, seq_lens, q_lat, q_rope):
        args = (c_raw.reshape(FULL[:4] + (4, 8, LATENT)), k_raw.transpose(1, 2, 0), rope_cos, rope_sin, norm_gain, seq_lens, q_lat, q_rope)
        c_cache, kr_turned, scores, lens = exchange(*[pltpu.with_memory_space_constraint(arg, pltpu.HBM) for arg in args])
        c_cache, kr_turned, o_lat = attend(c_cache.reshape(4, POSITIONS, LATENT), kr_turned, scores.reshape(POSITIONS, LANES), lens)
        return c_cache, kr_turned.transpose(0, 2, 1), o_lat

    return jax.shard_map(local_step, mesh=mesh, in_specs=(seq_spec, seq_spec, P(None), P("x", None), P("x", None), P("dp"), req_spec, req_spec), out_specs=(req_spec, req_spec, req_spec), check_vma=False)
```

time: 104 us -> 74.5 us (0.72); the launches traced: 102 us -> 74.3 us
  Pallas kernels: 0 us -> 73.7 us
  waiting for transfers between devices: 60.4 us -> 0 us
  starting transfers between devices: 17.9 us -> 0 us
  other arithmetic: 12.2 us -> 0 us
  local copies, waits for them, and re-layouts: 8.06 us -> 0 us
  matrix products: 3.02 us -> 0 us
    pallas_call x0 -> x2, Pallas kernels: none -> 73.7 us  [the longest x1 70.5 us: exchange(): pl.pallas_call(exchange_kernel, out_shape=[pltpu.VMEM((4, 4, 4, 4, 2, 8,...]
    all_to_all x2 -> x0, waiting for transfers between devices: 60.4 us -> none  [the longest x1 56.5 us: local_step(): c_cache = lax.all_to_all(c_norm, 'x', 0, 1, tiled=True)]
    all_to_all x2 -> x0, starting transfers between devices: 17.9 us -> none  [the longest x1 11.5 us: local_step(): kr_cache = lax.all_to_all(k_rope, 'x', 0, 1, tiled=True)]
    convert_element_type x4 -> x0, other arithmetic: 7.99 us -> none  [the longest x2 7.85 us: normed_rope(): return (c_norm.astype(jnp.bfloat16), k_rope.astype(jnp.bfloat16))]
    unnamed x18 -> x0, local copies, waits for them, and re-layouts: 5.01 us -> none
    reduce_sum x2 -> x0, other arithmetic: 3.29 us -> none  [the longest x1 3.09 us: normed_rope(): jnp.mean(lat_f32 * lat_f32, axis=-1, keepdims=True) + NORM_EPS]
    dot_general x3 -> x0, matrix products: 3.02 us -> none  [the longest x1 1.34 us: latent_attention(): jnp.einsum('rhs,rsk->rhk', weights.astype(jnp.bfloat16), c_cache, preferr...]
    all_to_all x2 -> x0, local copies, waits for them, and re-layouts: 2.76 us -> none  [the longest x1 2.58 us: local_step(): c_cache = lax.all_to_all(c_norm, 'x', 0, 1, tiled=True)]
  transfers between devices with their start and end apart: 2 -> 0, of which waited for: 2 -> 0; matrix products, arithmetic and copies ran while one was open for 11% -> 0% of each run, Pallas kernels for 0% -> 0%
where the time goes in v2:
time: 74.5 us; the launch traced here: 74.3 us
  Pallas kernels  73.7 us (99%)
    pallas_call x1, Pallas kernels, exchange(): pl.pallas_call(exchange_kernel, out_shape=[pltpu.VMEM((4, 4, 4, 4, 2, 8,...  70.5 us
    pallas_call x1, Pallas kernels, attend(): pl.pallas_call(attend_kernel, out_shape=[jax.ShapeDtypeStruct(c_cache.sha...  3.13 us

profile of v2, /device:TPU:1, one launch (start us, length us, event | category | flops | bytes accessed | tf_op | source)
XLA Modules:
  0.0 74.3 jit_solution(18020576852776516412)
XLA Ops:
  0.6 70.5 %exchange.1 = (bf16[4,4,4,4,2,8,512]{6,5,4,3,2,1,0:T(8,128)(2,1)S(1)}, bf16[4,64,1024]{2,1,0:T(8,128)(2,1)S(1)}, f32[4,4,4,2,8,128]{5,4,3,2,1,0:T(8,128)S(1)}, s32[8,128]{1,0:T(8,128)S(1)}) custom-call(bf16[4,4,4,2,4,8,512]{6,5,4,3,2,1,0:T(8,128)(2,1)} %bitcast.7, bf16[8,64,512]{2,1,0:T(8,128)(2,1)} %bitcast.8, f32[8,32]{1,0:T(8,128)} %cos_ref.1, ...), custom_call_target="tpu_custom_call" | custom-call | tf_op jit(solution)/shard_map/exchange/pallas_call | solution.py:370
  71.2 3.1 %attend.1 = (bf16[4,1024,512]{2,1,0:T(8,128)(2,1)}, bf16[4,64,1024]{2,1,0:T(8,128)(2,1)}, bf16[4,16,512]{2,1,0:T(8,128)(2,1)}) custom-call(bf16[4,1024,512]{2,1,0:T(8,128)(2,1)S(1)} %bitcast.5, bf16[4,64,1024]{2,1,0:T(8,128)(2,1)S(1)} %get-tuple-element.11.kr_ref, f32[1024,128]{1,0:T(8,128)S(1)} %bitcast.6, s32[8,128]{1,0:T(8,128)S(1)} %get-tuple-element.13.len_ref), custom_call_target="tpu_custom_call" | custom-call | tf_op jit(solution)/shard_map/attend/pallas_call | solution.py:405

commit v3 on v2

--- a/solution.py
+++ b/solution.py
@@ -19,8 +19,9 @@
 PAIR = range(2)
 REQUESTS = range(4)
 REQ = 512
-COPIES = 80
-LOADS = 27
+GROUPS = 28
+LOADS = 16
+SCORE_PARTS = 5
 SIGNS = (1, -1)
 OFFSETS = (0, -1, 1, 2)
 NT = (((1,), (1,)), ((), ()))
@@ -66,86 +67,89 @@
                 pl.semaphore_signal(barrier, inc=1, device_id={"x": device(dim, delta, k)}, device_id_type=pl.DeviceIdType.MESH)
     pl.semaphore_signal(barrier, inc=1, device_id={"x": other}, device_id_type=pl.DeviceIdType.MESH)
 
-    loads = {}
+    load_slots = {}
 
     def load(key, a, b):
-        copy = pltpu.make_async_copy(a, b, load_sem.at[len(loads)])
-        loads[key] = copy
+        slot = load_slots.setdefault(key, len(load_slots))
+        copy = pltpu.make_async_copy(a, b, load_sem.at[slot])
         copy.start()
-
-    def loaded(*keys):
-        for key in keys:
-            loads[key].wait()
+        return copy
 
     def load_slab(p, off, into, key):
         a = ORDERS[p][0]
         sel = {a: one(at(a, off))}
         rows = index(sel, COL - 1)
-        load((key, 0), c_ref.at[rows + (p, slice(None), pl.ds(*C_COLS))], view(into, {**sel, COL: C_COLS}))
+        load(key, c_ref.at[rows + (p, slice(None), pl.ds(*C_COLS))], view(into, {**sel, COL: C_COLS}))
         if p < 2:
-            load((key, 1), c_ref.at[rows + (3, slice(None), pl.ds(KEY_COLS * p, KEY_COLS))], view(into, {**sel, COL: K_COLS}))
-
-    load("k", k_ref, k_buf)
-    load("cos", cos_ref, cos_buf)
-    load("sin", sin_ref, sin_buf)
-    for off in (2, 1, -1):
-        for p in PARTS:
-            load_slab(p, off, src[p], ("src", p, off))
+            load(key, c_ref.at[rows + (3, slice(None), pl.ds(KEY_COLS * p, KEY_COLS))], view(into, {**sel, COL: K_COLS}))
+
+    def taken(sem, shape):
+        pltpu.make_async_copy(view(got[0], shape), view(got[0], shape), sem).wait()
+
+    def slabs(p, n):
+        return {ORDERS[p][0]: (0, n), COL: ALL_COLS if p < 2 else C_COLS}
+
+    def loaded(key, p, n):
+        taken(load_sem.at[load_slots[key, p]], slabs(p, n))
+
+    key_loads = [load("k", k_ref, k_buf), load("cos", cos_ref, cos_buf), load("sin", sin_ref, sin_buf)]
+    for p in PARTS:
+        load_slab(p, 2, src[p], ("far", p))
+    for p in PARTS:
+        for sign in SIGNS:
+            load_slab(p, sign, src[p], ("near", p))
     for p in PARTS:
         load_slab(p, 0, mid1[p], ("own", p))
-    load("gain", gain_ref, gain_buf)
-    load("len", len_ref, len_buf)
-    load("qlat", qlat_ref, qlat_buf)
-    load("qrope", qrope_ref, qrope_buf)
-
-    copies = [{} for _ in PARTS]
-
-    def send(p, key, a, b, to):
-        n = len(copies[p])
-        copy = pltpu.make_async_remote_copy(src_ref=a, dst_ref=b, send_sem=send_sem.at[p, n], recv_sem=recv_sem.at[p, n], device_id={"x": to}, device_id_type=pl.DeviceIdType.MESH)
-        copies[p][key] = copy
-        copy.start()
-
-    def arrived(p, *keys):
-        for key in keys:
-            copies[p][key].wait_recv()
-
-    def phase1(p, cols=ALL_COLS):
+    other_loads = [load("gain", gain_ref, gain_buf), load("len", len_ref, len_buf), load("qlat", qlat_ref, qlat_buf), load("qrope", qrope_ref, qrope_buf)]
+
+    slots = [{} for _ in PARTS]
+
+    def send(p, group, a, b, to, sent):
+        slot = slots[p].setdefault(group, len(slots[p]))
+        pltpu.make_async_remote_copy(src_ref=a, dst_ref=b, send_sem=send_sem.at[p, sent], recv_sem=recv_sem.at[p, slot], device_id={"x": to}, device_id_type=pl.DeviceIdType.MESH).start()
+
+    def arrived(p, group, shape):
+        taken(recv_sem.at[p, slots[p][group]], shape)
+
+    def far1(p, cols=ALL_COLS):
         a, b, _ = ORDERS[p]
         wide = {COL: cols}
         for s, sign in enumerate(SIGNS):
-            send(p, ("1far", cols, s), view(src[p], {a: one(at(a, 2)), b: halves(s), **wide}), view(hop1[2 * p + s], wide), device(a, sign))
-        for s, sign in enumerate(SIGNS):
-            send(p, ("1near", cols, s), view(src[p], {a: one(at(a, sign)), **wide}), view(mid1[p], {a: one(place[a]), **wide}), device(a, sign))
+            send(p, ("1far", cols), view(src[p], {a: one(at(a, 2)), b: halves(s), **wide}), view(hop1[2 * p + s], wide), device(a, sign), 0)
+
+    def near1(p, cols=ALL_COLS):
+        a, b, _ = ORDERS[p]
+        wide = {COL: cols}
+        for s, sign in enumerate(SIGNS):
+            send(p, ("1near", cols), view(src[p], {a: one(at(a, sign)), **wide}), view(mid1[p], {a: one(place[a]), **wide}), device(a, sign), 0)
 
     def forward1(p, cols=ALL_COLS):
         a, b, _ = ORDERS[p]
         wide = {COL: cols}
-        for s, sign in enumerate(SIGNS):
-            arrived(p, ("1far", cols, s))
-            send(p, ("1fwd", cols, s), view(hop1[2 * p + s], wide), view(mid1[p], {a: one(at(a, -sign)), b: halves(s), **wide}), device(a, sign))
-
-    def arrived1(p, kind):
-        for key in list(copies[p]):
-            if key[0] == kind:
-                arrived(p, key)
+        arrived(p, ("1far", cols), {a: one(0), **wide})
+        for s, sign in enumerate(SIGNS):
+            send(p, ("1fwd", cols), view(hop1[2 * p + s], wide), view(mid1[p], {a: one(at(a, -sign)), b: halves(s), **wide}), device(a, sign), 0)
+
+    def arrived1(p, kind, n):
+        for cols in (ALL_COLS,) if p < 2 else (C_COLS, K_COLS):
+            arrived(p, (kind, cols), {ORDERS[p][0]: (0, n), COL: cols})
 
     def phase2(p, off):
         a, b, c = ORDERS[p]
         sa = {a: one(at(a, off))}
         hop_sa = {a: one(off % 4)}
         for s, sign in enumerate(SIGNS):
-            send(p, ("2far", off, s), view(mid1[p], {**sa, b: one(at(b, 2)), c: halves(s)}), view(hop2[2 * p + s], hop_sa), device(b, sign))
-        for s, sign in enumerate(SIGNS):
-            send(p, ("2near", off, s), view(mid1[p], {**sa, b: one(at(b, sign))}), view(mid2[p], {**sa, b: one(place[b])}), device(b, sign))
+            send(p, ("2far", off), view(mid1[p], {**sa, b: one(at(b, 2)), c: halves(s)}), view(hop2[2 * p + s], hop_sa), device(b, sign), 1)
+        for s, sign in enumerate(SIGNS):
+            send(p, "2near", view(mid1[p], {**sa, b: one(at(b, sign))}), view(mid2[p], {**sa, b: one(place[b])}), device(b, sign), 1)
 
     def forward2(p, off):
         a, b, c = ORDERS[p]
         sa = {a: one(at(a, off))}
         hop_sa = {a: one(off % 4)}
-        for s, sign in enumerate(SIGNS):
-            arrived(p, ("2far", off, s))
-            send(p, ("2fwd", off, s), view(hop2[2 * p + s], hop_sa), view(mid2[p], {**sa, b: one(at(b, -sign)), c: halves(s)}), device(b, sign))
+        arrived(p, ("2far", off), {a: one(0), b: one(0)})
+        for s, sign in enumerate(SIGNS):
+            send(p, "2fwd", view(hop2[2 * p + s], hop_sa), view(mid2[p], {**sa, b: one(at(b, -sign)), c: halves(s)}), device(b, sign), 1)
 
     def phase3(p, off):
         a, b, c = ORDERS[p]
@@ -154,20 +158,20 @@
         held = mid1[p] if off == 0 else mid2[p]
         mine = {**sb, c: one(place[c]), CORE: one(core)}
         for s, sign in enumerate(SIGNS):
-            send(p, ("3far", off, s), view(held, {**sb, c: one(at(c, 2)), CORE: one(cores[s])}), view(hop3[2 * p + s], hop_sb), device(c, sign))
+            send(p, ("3far", off), view(held, {**sb, c: one(at(c, 2)), CORE: one(cores[s])}), view(hop3[2 * p + s], hop_sb), device(c, sign), 2)
         for s, sign in enumerate(SIGNS):
             for k in PAIR:
-                send(p, ("3near", off, s, k), view(held, {**sb, c: one(at(c, sign)), CORE: one(cores[k])}), view(got[p], mine), device(c, sign, cores[k]))
-        send(p, ("3core", off), view(held, {**sb, c: one(place[c]), CORE: one(cores[1])}), view(got[p], mine), other)
+                send(p, ("3near", off), view(held, {**sb, c: one(at(c, sign)), CORE: one(cores[k])}), view(got[p], mine), device(c, sign, cores[k]), 2)
+        send(p, ("3core", off), view(held, {**sb, c: one(place[c]), CORE: one(cores[1])}), view(got[p], mine), other, 3)
         got[p][index(mine)] = held[index(mine)]
 
     def forward3(p, off):
         a, b, c = ORDERS[p]
         sb = {b: one(at(b, off))}
         hop_sb = {b: one(off % 4)}
-        for s, sign in enumerate(SIGNS):
-            arrived(p, ("3far", off, s))
-            send(p, ("3fwd", off, s), view(hop3[2 * p + s], hop_sb), view(got[p], {**sb, c: one(at(c, -sign)), CORE: one(core)}), device(c, sign, cores[s]))
+        arrived(p, ("3far", off), {b: one(0), c: one(0)})
+        for s, sign in enumerate(SIGNS):
+            send(p, ("3fwd", off), view(hop3[2 * p + s], hop_sb), view(got[p], {**sb, c: one(at(c, -sign)), CORE: one(core)}), device(c, sign, cores[s]), 2)
 
     def length(j):
         return len_buf[4 * me + j]
@@ -204,7 +208,6 @@
         qk_rows[...] = jnp.zeros_like(qk_rows)
         for j in REQUESTS:
             qk_rows[HEADS * j : HEADS * (j + 1), :] = jnp.concatenate([qrope_buf[j] if i == j else zero for i in REQUESTS], axis=1)
-        score_out[...] = jnp.zeros_like(score_out)
         lane = lax.broadcasted_iota(jnp.int32, (8, LANES), 1)
         lens = jnp.zeros((8, LANES), jnp.int32)
         for j in REQUESTS:
@@ -224,7 +227,7 @@
         c_norm = raw * inv_rms * gain
         c_out[(j,) + where] = c_norm.reshape(unit_shape(a, LATENT)).astype(BF16)
         part = lax.dot_general(c_norm.astype(BF16), q_rows[j], NT, preferred_element_type=F32)
-        score_out[where] += part.reshape(unit_shape(a, LANES))
+        score_out[(j,) + where] = part.reshape(unit_shape(a, LANES))
 
     def gain_row():
         return gain_buf[...].astype(F32).reshape(1, LATENT)
@@ -238,19 +241,18 @@
         if p == 2:
             held = got[2][where + (pl.ds(*K_COLS),)].astype(F32).reshape(ROWS, KEY_COLS).astype(BF16)
             part = lax.dot_general(held, qk_rows[...], NT, preferred_element_type=F32)
-            score_out[where + (slice(None),)] += part.reshape(unit_shape(a, LANES))
+            score_out[(4,) + where + (slice(None),)] = part.reshape(unit_shape(a, LANES))
 
     def near_units(p, off):
         a, b, c = ORDERS[p]
-        arrived(p, ("3core", off), *[("3near", off, s, k) for s in PAIR for k in PAIR])
-
-        @pl.loop(0, 3)
-        def _(i):
-            unit(p, at(b, off), (place[c] + 3 + i) % 4)
+        arrived(p, ("3near", off), {b: one(0), c: (0, 2)})
+        arrived(p, ("3core", off), {b: one(0), c: one(0), CORE: one(0)})
+        for step in OFFSETS[:3]:
+            unit(p, at(b, off), at(c, step))
 
     def far_unit(p, off):
         a, b, c = ORDERS[p]
-        arrived(p, ("3fwd", off, 0), ("3fwd", off, 1))
+        arrived(p, ("3fwd", off), {b: one(0), c: one(0)})
         unit(p, at(b, off), at(c, 2))
         if p == 2:
             key_columns(at(b, off))
@@ -265,33 +267,37 @@
             valid = col[:ROPE] + z * KEY_COLS < length(j)
             kr_out[j, :, pl.ds(pl.multiple_of(z * KEY_COLS, KEY_COLS), KEY_COLS)] = jnp.where(valid, turned[ROPE * j : ROPE * (j + 1)], 0.0).astype(BF16)
 
-    def last_request():
-        @pl.loop(0, 16)
-        def _(i):
-            y, x = i // 4, i % 4
+    def last_request(blocks):
+        for off_y, off_x in blocks:
+            y, x = at(1, off_y), at(2, off_x)
             where = index({1: one(y), 2: one(x)})[:COL]
             gain = gain_row()
             raw = [got[p][where + (pl.ds(*K_COLS),)].astype(F32).reshape(ROWS, KEY_COLS) for p in PAIR]
             finish_rows(3, jnp.concatenate(raw, axis=1), gain, row_positions(0, 1, 2, y, x), 0, where + (slice(None),))
 
-    for off in (2, 1, -1):
-        for p in PARTS:
-            loaded((("src", p, off), 0))
-            if p < 2:
-                loaded((("src", p, off), 1))
+    def blocks(n):
+        inner = OFFSETS[: n - 1]
+        return [(y, x) for y in OFFSETS[:n] for x in OFFSETS[:n] if y not in inner or x not in inner]
+
+    for p in PARTS:
+        loaded("far", p, 1)
     pl.semaphore_wait(barrier, 13)
-    phase1(0)
-    phase1(1)
-    phase1(2, C_COLS)
-    loaded("k", "cos", "sin")
+    far1(0)
+    far1(1)
+    far1(2, C_COLS)
+    for p in PARTS:
+        loaded("near", p, 2)
+        near1(p, ALL_COLS if p < 2 else C_COLS)
+    for copy in key_loads:
+        copy.wait()
     keys()
-    loaded("gain", "len", "qlat", "qrope")
+    for copy in other_loads:
+        copy.wait()
     queries()
-    phase1(2, K_COLS)
-    for p in PARTS:
-        loaded((("own", p), 0))
-        if p < 2:
-            loaded((("own", p), 1))
+    far1(2, K_COLS)
+    near1(2, K_COLS)
+    for p in PARTS:
+        loaded("own", p, 1)
     forward1(0)
     forward1(1)
     forward1(2, C_COLS)
@@ -299,13 +305,13 @@
         phase2(p, 0)
     forward1(2, K_COLS)
     for p in PARTS:
-        arrived1(p, "1near")
+        arrived1(p, "1near", 2)
         phase2(p, -1)
         phase2(p, 1)
     for p in PARTS:
         forward2(p, 0)
     for p in PARTS:
-        arrived1(p, "1fwd")
+        arrived1(p, "1fwd", 1)
         phase2(p, 2)
     for p in PARTS:
         forward2(p, -1)
@@ -314,8 +320,7 @@
         forward2(p, 2)
         phase3(p, 0)
     for p in PARTS:
-        for off in OFFSETS:
-            arrived(p, ("2near", off, 0), ("2near", off, 1))
+        arrived(p, "2near", {ORDERS[p][1]: (0, 2)})
         phase3(p, -1)
     for p in PARTS:
         forward3(p, 0)
@@ -323,8 +328,7 @@
     for p in PARTS:
         near_units(p, 0)
     for p in PARTS:
-        for off in OFFSETS:
-            arrived(p, ("2fwd", off, 0), ("2fwd", off, 1))
+        arrived(p, "2fwd", {ORDERS[p][1]: one(0)})
         forward3(p, -1)
         phase3(p, 2)
     for p in PARTS:
@@ -335,17 +339,21 @@
     for p in PARTS:
         near_units(p, 1)
         far_unit(p, -1)
+    last_request(blocks(1) + blocks(2))
     for p in PARTS:
         forward3(p, 2)
     for p in PARTS:
         near_units(p, 2)
         far_unit(p, 1)
+    last_request(blocks(3))
     for p in PARTS:
         far_unit(p, 2)
-    last_request()
-    for p in PARTS:
-        for copy in copies[p].values():
-            copy.wait_send()
+    last_request(blocks(4))
+    for p in PARTS:
+        c = ORDERS[p][2]
+        for phase in PARTS:
+            taken(send_sem.at[p, phase], {})
+        taken(send_sem.at[p, 3], {c: one(0), CORE: one(0)})
 
 
 def exchange(c_raw, k_turned, rope_cos, rope_sin, gain, seq_lens, q_lat, q_rope):
@@ -366,13 +374,13 @@
         pltpu.VMEM((4, 128, 512), BF16),
         pltpu.VMEM((128, 256), BF16),
     ]
-    sems = [pltpu.SemaphoreType.DMA((LOADS,)), pltpu.SemaphoreType.DMA((3, COPIES)), pltpu.SemaphoreType.DMA((3, COPIES))]
+    sems = [pltpu.SemaphoreType.DMA((LOADS,)), pltpu.SemaphoreType.DMA((3, 4)), pltpu.SemaphoreType.DMA((3, GROUPS))]
     return pl.pallas_call(
         exchange_kernel,
         out_shape=[
             pltpu.VMEM((4, 4, 4, 4, 2, 8, 512), BF16),
             pltpu.VMEM((4, 64, 1024), BF16),
-            pltpu.VMEM((4, 4, 4, 2, 8, 128), F32),
+            pltpu.VMEM((SCORE_PARTS,) + FULL[:COL] + (LANES,), F32),
             pltpu.VMEM((8, LANES), jnp.int32),
         ],
         in_specs=[pl.BlockSpec(memory_space=pltpu.HBM)] * 8,
@@ -388,7 +396,7 @@
     for write in writes:
         write.start()
     row = lax.broadcasted_iota(jnp.int32, (POSITIONS, LANES), 0)
-    scores = jnp.where(row < len_ref[0:1, :], score_ref[...] * ATTN_SCALE, -1e30)
+    scores = jnp.where(row < len_ref[0:1, :], jnp.sum(score_ref[...], axis=0) * ATTN_SCALE, -1e30)
     weights = jnp.exp(scores - jnp.max(scores, axis=0, keepdims=True)).T
     weight_sum = jnp.sum(weights[: 4 * HEADS], axis=1, keepdims=True)
     rounded = weights[: 4 * HEADS].astype(BF16)
@@ -424,7 +432,7 @@
     def local_step(c_raw, k_raw, norm_gain, rope_cos, rope_sin, seq_lens, q_lat, q_rope):
         args = (c_raw.reshape(FULL[:4] + (4, 8, LATENT)), k_raw.transpose(1, 2, 0), rope_cos, rope_sin, norm_gain, seq_lens, q_lat, q_rope)
         c_cache, kr_turned, scores, lens = exchange(*[pltpu.with_memory_space_constraint(arg, pltpu.HBM) for arg in args])
-        c_cache, kr_turned, o_lat = attend(c_cache.reshape(4, POSITIONS, LATENT), kr_turned, scores.reshape(POSITIONS, LANES), lens)
+        c_cache, kr_turned, o_lat = attend(c_cache.reshape(4, POSITIONS, LATENT), kr_turned, scores.reshape(SCORE_PARTS, POSITIONS, LANES), lens)
         return c_cache, kr_turned.transpose(0, 2, 1), o_lat
 
     return jax.shard_map(local_step, mesh=mesh, in_specs=(seq_spec, seq_spec, P(None), P("x", None), P("x", None), P("dp"), req_spec, req_spec), out_specs=(req_spec, req_spec, req_spec), check_vma=False)

time: 74.5 us -> 66.5 us (0.89)
  Pallas kernels: 73.7 us -> 65.1 us
    pallas_call x1, Pallas kernels: 70.5 us -> 61.9 us  [exchange(): pl.pallas_call(exchange_kernel, out_shape=[pltpu.VMEM((4, 4, 4, 4, 2, 8,...]
where the time goes in v3:
time: 66.5 us; the launch traced here: 65.7 us
  Pallas kernels  65.1 us (98%)
    pallas_call x1, Pallas kernels, exchange(): pl.pallas_call(exchange_kernel, out_shape=[pltpu.VMEM((4, 4, 4, 4, 2, 8,...  61.9 us
    pallas_call x1, Pallas kernels, attend(): pl.pallas_call(attend_kernel, out_shape=[jax.ShapeDtypeStruct(c_cache.sha...  3.17 us

profile of v3, /device:TPU:1, one launch (start us, length us, event | category | flops | bytes accessed | tf_op | source)
XLA Modules:
  0.0 65.7 jit_solution(10835998186922330904)
XLA Ops:
  0.6 61.9 %exchange.1 = (bf16[4,4,4,4,2,8,512]{6,5,4,3,2,1,0:T(8,128)(2,1)S(1)}, bf16[4,64,1024]{2,1,0:T(8,128)(2,1)S(1)}, f32[5,4,4,4,2,8,128]{6,5,4,3,2,1,0:T(8,128)S(1)}, s32[8,128]{1,0:T(8,128)S(1)}) custom-call(bf16[4,4,4,2,4,8,512]{6,5,4,3,2,1,0:T(8,128)(2,1)} %bitcast.7, bf16[8,64,512]{2,1,0:T(8,128)(2,1)} %bitcast.8, f32[8,32]{1,0:T(8,128)} %cos_ref.1, ...), custom_call_target="tpu_custom_call" | custom-call | tf_op jit(solution)/shard_map/exchange/pallas_call | solution.py:378
  62.6 3.2 %attend.1 = (bf16[4,1024,512]{2,1,0:T(8,128)(2,1)}, bf16[4,64,1024]{2,1,0:T(8,128)(2,1)}, bf16[4,16,512]{2,1,0:T(8,128)(2,1)}) custom-call(bf16[4,1024,512]{2,1,0:T(8,128)(2,1)S(1)} %bitcast.5, bf16[4,64,1024]{2,1,0:T(8,128)(2,1)S(1)} %get-tuple-element.11.kr_ref, f32[5,1024,128]{2,1,0:T(8,128)S(1)} %bitcast.6, s32[8,128]{1,0:T(8,128)S(1)} %get-tuple-element.13.len_ref), custom_call_target="tpu_custom_call" | custom-call | tf_op jit(solution)/shard_map/attend/pallas_call | solution.py:413

commit v4 on v3

v4 whole, which is shorter than its diff:
```python
import jax
import jax.numpy as jnp
from jax import lax
from jax.experimental import pallas as pl
from jax.experimental.pallas import tpu as pltpu
from jax.sharding import PartitionSpec as P

NORM_EPS = 1e-6
ATTN_SCALE = (512 + 64) ** -0.5
ORDERS = ((0, 1, 2), (1, 2, 0), (2, 0, 1))
FULL = (4, 4, 4, 2, 8, 768)
STRIDES = (256, 64, 16)
POSITIONS, LATENT, ROPE, HEADS, LANES = 1024, 512, 64, 16, 128
ROWS = 64
KEY_COLS = 256
C_COLS, K_COLS, ALL_COLS = (0, LATENT), (LATENT, KEY_COLS), (0, LATENT + KEY_COLS)
CORE, COL = 3, 5
PARTS = range(3)
PAIR = range(2)
REQUESTS = range(4)
REQ = 512
GROUPS = 23
LOADS = 9
SCORE_PARTS = 5
SIGNS = (1, -1)
OFFSETS = (0, -1, 1, 2)
NT = (((1,), (1,)), ((), ()))
F32, BF16 = jnp.float32, jnp.bfloat16


def exchange_kernel(c_ref, k_ref, cos_ref, sin_ref, gain_ref, len_ref, qlat_ref, qrope_ref, c_out, kr_out, score_out, len_out, scratch):
    parts, k_laid, hop1, hop2, hop3, small, sems = scratch
    mid1, mid2, got = [[parts.at[3 * stage + p] for p in PARTS] for stage in PARTS]
    k_buf, cos_buf, sin_buf, gain_buf, len_buf, qlat_buf, qrope_buf, q_rows, qk_rows = small
    load_sem, send_sem, recv_sem = sems

    me = lax.axis_index("x")
    core = me % 2
    other = me + 1 - 2 * core
    cores = (core, 1 - core)
    place = (me // 32, (me // 8) % 4, (me // 2) % 4)

    def device(dim, delta, to_core=None):
        pos = list(place)
        pos[dim] = (pos[dim] + delta + 4) % 4
        last = core if to_core is None else to_core
        return ((pos[0] * 4 + pos[1]) * 4 + pos[2]) * 2 + last

    def at(dim, delta):
        return (place[dim] + delta + 4) % 4

    def index(sel, dims=len(FULL)):
        return tuple(pl.ds(*sel[d]) if d in sel else slice(None) for d in range(dims))

    def one(i):
        return (i, 1)

    def halves(s):
        return (2 * s, 2)

    def view(ref, sel):
        return ref.at[index(sel)]

    barrier = pltpu.get_barrier_semaphore()
    for dim in PARTS:
        for delta in SIGNS:
            for k in PAIR:
                pl.semaphore_signal(barrier, inc=1, device_id={"x": device(dim, delta, k)}, device_id_type=pl.DeviceIdType.MESH)
    pl.semaphore_signal(barrier, inc=1, device_id={"x": other}, device_id_type=pl.DeviceIdType.MESH)

    def taken(sem, n, shape):
        block = parts.at[(pl.ds(0, n),) + index(shape)]
        pltpu.make_async_copy(block, block, sem).wait()

    def taken_from(p, sel, extra):
        where = index(sel, COL - 1)
        if extra:
            return c_ref.at[where + (3, slice(None), pl.ds(KEY_COLS * p, KEY_COLS))]
        return c_ref.at[where + (p, slice(None), pl.ds(*C_COLS))]

    def load(slot, a, b):
        copy = pltpu.make_async_copy(a, b, load_sem.at[slot])
        copy.start()
        return copy

    key_loads = [load(i, a, b) for i, (a, b) in enumerate(((k_ref, k_buf), (cos_ref, cos_buf), (sin_ref, sin_buf)))]
    other_loads = [load(3 + i, a, b) for i, (a, b) in enumerate(((gain_ref, gain_buf), (len_ref, len_buf), (qlat_ref, qlat_buf), (qrope_ref, qrope_buf)))]
    for p in PARTS:
        own = {ORDERS[p][0]: one(place[ORDERS[p][0]])}
        load(LOADS - 1 if p == 2 else LOADS - 2, taken_from(p, own, False), view(mid1[p], {**own, COL: C_COLS}))
        if p < 2:
            load(LOADS - 2, taken_from(p, own, True), view(mid1[p], {**own, COL: K_COLS}))

    slots = {}

    def send(group, a, b, to, sent=0):
        slot = slots.setdefault(group, len(slots))
        pltpu.make_async_remote_copy(src_ref=a, dst_ref=b, send_sem=send_sem.at[sent], recv_sem=recv_sem.at[slot], device_id={"x": to}, device_id_type=pl.DeviceIdType.MESH).start()

    def arrived(group, n, shape):
        taken(recv_sem.at[slots[group]], n, shape)

    def held(p, sel, cols):
        if cols == C_COLS:
            return taken_from(p, sel, False)
        return taken_from(p, sel, True) if p < 2 else view(k_laid, sel)

    def first_group(p, cols):
        return ("1far", cols if p == 2 else None)

    def far1(p, cols):
        a, b, _ = ORDERS[p]
        wide = {COL: cols}
        for s, sign in enumerate(SIGNS):
            send(first_group(p, cols), held(p, {a: one(at(a, 2)), b: halves(s)}, cols), view(hop1[2 * p + s], wide), device(a, sign))

    def near1(p, cols):
        a, b, _ = ORDERS[p]
        wide = {COL: cols}
        for s, sign in enumerate(SIGNS):
            send("1near", held(p, {a: one(at(a, sign))}, cols), view(mid1[p], {a: one(place[a]), **wide}), device(a, sign))

    def forward1(p, cols=ALL_COLS):
        a, b, _ = ORDERS[p]
        wide = {COL: cols}
        for s, sign in enumerate(SIGNS):
            send("1fwd", view(hop1[2 * p + s], wide), view(mid1[p], {a: one(at(a, -sign)), b: halves(s), **wide}), device(a, sign))

    def phase2(p, off):
        a, b, c = ORDERS[p]
        sa = {a: one(at(a, off))}
        hop_sa = {a: one(off % 4)}
        for s, sign in enumerate(SIGNS):
            send(("2far", off), view(mid1[p], {**sa, b: one(at(b, 2)), c: halves(s)}), view(hop2[2 * p + s], hop_sa), device(b, sign))
        for s, sign in enumerate(SIGNS):
            send("2near", view(mid1[p], {**sa, b: one(at(b, sign))}), view(mid2[p], {**sa, b: one(place[b])}), device(b, sign))

    def forward2(p, off):
        a, b, c = ORDERS[p]
        sa = {a: one(at(a, off))}
        hop_sa = {a: one(off % 4)}
        for s, sign in enumerate(SIGNS):
            send("2fwd", view(hop2[2 * p + s], hop_sa), view(mid2[p], {**sa, b: one(at(b, -sign)), c: halves(s)}), device(b, sign))

    def phase3(p, off):
        a, b, c = ORDERS[p]
        sb = {b: one(at(b, off))}
        hop_sb = {b: one(off % 4)}
        got_b = mid1[p] if off == 0 else mid2[p]
        mine = {**sb, c: one(place[c]), CORE: one(core)}
        for s, sign in enumerate(SIGNS):
            send(("3far", off), view(got_b, {**sb, c: one(at(c, 2)), CORE: one(cores[s])}), view(hop3[2 * p + s], hop_sb), device(c, sign))
        for s, sign in enumerate(SIGNS):
            for k in PAIR:
                send(("3near", off), view(got_b, {**sb, c: one(at(c, sign)), CORE: one(cores[k])}), view(got[p], mine), device(c, sign, cores[k]))
        send(("3near", off), view(got_b, {**sb, c: one(place[c]), CORE: one(cores[1])}), view(got[p], mine), other, 1)
        got[p][index(mine)] = got_b[index(mine)]

    def forward3(p, off):
        a, b, c = ORDERS[p]
        sb = {b: one(at(b, off))}
        hop_sb = {b: one(off % 4)}
        for s, sign in enumerate(SIGNS):
            send(("3fwd", off), view(hop3[2 * p + s], hop_sb), view(got[p], {**sb, c: one(at(c, -sign)), CORE: one(core)}), device(c, sign, cores[s]))

    def length(j):
        return len_buf[4 * me + j]

    def keys():
        row = lax.broadcasted_iota(jnp.int32, (32, 32), 0)
        diag = row == lax.broadcasted_iota(jnp.int32, (32, 32), 1)
        roped = []
        for pos in range(8):
            cos = jnp.sum(jnp.where(diag, cos_buf[pos : pos + 1, :], 0.0), axis=1, keepdims=True)
            sin = jnp.sum(jnp.where(diag, sin_buf[pos : pos + 1, :], 0.0), axis=1, keepdims=True)
            lo = k_buf[pos, 0:32, :].astype(F32)
            hi = k_buf[pos, 32:64, :].astype(F32)
            roped.append(jnp.concatenate([lo * cos - hi * sin, hi * cos + lo * sin], axis=0).astype(BF16))
        out_row = lax.broadcasted_iota(jnp.int32, (256, 128), 0)
        lane = lax.broadcasted_iota(jnp.int32, (256, 128), 1)
        picks = [jnp.where((out_row % 8 == pos) & (out_row // 8 == lane // 4), 1.0, 0.0).astype(BF16) for pos in range(8)]
        pick = jnp.concatenate(picks, axis=1)
        request = lax.broadcasted_iota(jnp.int32, (64, 1024), 1) % 4
        for z in REQUESTS:
            cat = jnp.concatenate([r[:, 128 * z : 128 * (z + 1)] for r in roped], axis=1)
            masked = jnp.concatenate([jnp.where(request == j, cat, jnp.zeros_like(cat)) for j in REQUESTS], axis=0)
            laid = lax.dot_general(pick, masked, NT, preferred_element_type=F32)
            laid = laid.reshape(1, 4, 4, 2, 8, 256).astype(BF16)
            k_laid[z : z + 1] = laid
        own = {2: one(place[2])}
        mid1[2][index({**own, COL: K_COLS})] = k_laid[index(own)]

    def queries():
        q_rows[...] = jnp.zeros_like(q_rows)
        for j in REQUESTS:
            q_rows[j, HEADS * j : HEADS * (j + 1), :] = qlat_buf[j]
        zero = jnp.zeros((HEADS, ROPE), BF16)
        qk_rows[...] = jnp.zeros_like(qk_rows)
        for j in REQUESTS:
            qk_rows[HEADS * j : HEADS * (j + 1), :] = jnp.concatenate([qrope_buf[j] if i == j else zero for i in REQUESTS], axis=1)
        lane = lax.broadcasted_iota(jnp.int32, (8, LANES), 1)
        lens = jnp.zeros((8, LANES), jnp.int32)
        for j in REQUESTS:
            lens = jnp.where(lane // HEADS == j, length(j), lens)
        len_out[...] = lens

    def row_positions(a, b, c, ib, ic):
        r = lax.broadcasted_iota(jnp.int32, (ROWS, 1), 0)
        return (r // 16) * STRIDES[a] + r % 16 + ib * STRIDES[b] + ic * STRIDES[c]

    def unit_shape(a, width):
        return tuple(4 if d == a else 1 for d in range(3)) + (2, 8, width)

    def finish_rows(j, raw, gain, positions, a, where):
        square = jnp.sum(raw * raw, axis=-1, keepdims=True) * (1.0 / 512)
        inv_rms = jnp.where(positions < length(j), lax.rsqrt(square + NORM_EPS), 0.0)
        c_norm = raw * inv_rms * gain
        c_out[(j,) + where] = c_norm.reshape(unit_shape(a, LATENT)).astype(BF16)
        part = lax.dot_general(c_norm.astype(BF16), q_rows[j], NT, preferred_element_type=F32)
        score_out[(j,) + where] = part.reshape(unit_shape(a, LANES))

    def gain_row():
        return gain_buf[...].astype(F32).reshape(1, LATENT)

    def unit(p, ib, ic):
        a, b, c = ORDERS[p]
        where = index({b: one(ib), c: one(ic)})[:COL]
        gain = gain_row()
        raw = got[p][where + (pl.ds(*C_COLS),)].astype(F32).reshape(ROWS, LATENT)
        finish_rows(p, raw, gain, row_positions(a, b, c, ib, ic), a, where + (slice(None),))
        if p == 2:
            tile = got[2][where + (pl.ds(*K_COLS),)].astype(F32).reshape(ROWS, KEY_COLS).astype(BF16)
            part = lax.dot_general(tile, qk_rows[...], NT, preferred_element_type=F32)
            score_out[(4,) + where + (slice(None),)] = part.reshape(unit_shape(a, LANES))

    def near_units(off):
        arrived(("3near", off), 5, {0: (0, 3), 1: one(0), CORE: one(0)})
        for p in PARTS:
            _, b, c = ORDERS[p]
            for step in OFFSETS[:3]:
                unit(p, at(b, off), at(c, step))

    def far_units(off):
        arrived(("3fwd", off), 3, {0: one(0), 1: one(0)})
        for p in PARTS:
            _, b, c = ORDERS[p]
            unit(p, at(b, off), at(c, 2))
        key_columns(at(ORDERS[2][1], off))

    def key_columns(z):
        row = lax.broadcasted_iota(jnp.int32, (KEY_COLS, KEY_COLS), 0)
        col = lax.broadcasted_iota(jnp.int32, (KEY_COLS, KEY_COLS), 1)
        eye = jnp.where(row == col, 1.0, 0.0).astype(BF16)
        tile = got[2][pl.ds(z, 1), :, :, :, :, pl.ds(*K_COLS)].astype(F32).reshape(KEY_COLS, KEY_COLS).astype(BF16)
        turned = lax.dot_general(eye, tile, NT, preferred_element_type=F32)
        for j in REQUESTS:
            valid = col[:ROPE] + z * KEY_COLS < length(j)
            kr_out[j, :, pl.ds(pl.multiple_of(z * KEY_COLS, KEY_COLS), KEY_COLS)] = jnp.where(valid, turned[ROPE * j : ROPE * (j + 1)], 0.0).astype(BF16)

    def last_request(blocks):
        for off_y, off_x in blocks:
            y, x = at(1, off_y), at(2, off_x)
            where = index({1: one(y), 2: one(x)})[:COL]
            gain = gain_row()
            raw = [got[p][where + (pl.ds(*K_COLS),)].astype(F32).reshape(ROWS, KEY_COLS) for p in PAIR]
            finish_rows(3, jnp.concatenate(raw, axis=1), gain, row_positions(0, 1, 2, y, x), 0, where + (slice(None),))

    def blocks(n):
        inner = OFFSETS[: n - 1]
        return [(y, x) for y in OFFSETS[:n] for x in OFFSETS[:n] if y not in inner or x not in inner]

    def all_parts(step, *args):
        for p in PARTS:
            step(p, *args)

    EIGHTH, SIXTEENTH = {0: one(0), 1: (0, 2)}, {0: one(0), 1: one(0)}
    pl.semaphore_wait(barrier, 13)
    for first in (far1, near1):
        all_parts(first, C_COLS)
        first(0, K_COLS)
        first(1, K_COLS)
    for copy in key_loads:
        copy.wait()
    keys()
    for copy in other_loads:
        copy.wait()
    queries()
    far1(2, K_COLS)
    near1(2, K_COLS)
    taken(load_sem.at[LOADS - 2], 2, {0: one(0)})
    taken(load_sem.at[LOADS - 1], 1, {0: one(0), COL: C_COLS})
    arrived(first_group(0, None), 2, {0: one(0)})
    forward1(0)
    forward1(1)
    arrived(first_group(2, C_COLS), 1, {0: one(0), COL: C_COLS})
    forward1(2, C_COLS)
    all_parts(phase2, 0)
    arrived(first_group(2, K_COLS), 1, {0: one(0), COL: K_COLS})
    forward1(2, K_COLS)
    arrived("1near", 3, {0: (0, 2)})
    all_parts(phase2, -1)
    all_parts(phase2, 1)
    arrived(("2far", 0), 3, SIXTEENTH)
    all_parts(forward2, 0)
    arrived("1fwd", 3, {0: one(0)})
    all_parts(phase2, 2)
    for off in (-1, 1):
        arrived(("2far", off), 3, SIXTEENTH)
        all_parts(forward2, off)
    arrived(("2far", 2), 3, SIXTEENTH)
    all_parts(forward2, 2)
    all_parts(phase3, 0)
    arrived("2near", 3, {0: (0, 2)})
    all_parts(phase3, -1)
    arrived(("3far", 0), 3, SIXTEENTH)
    all_parts(forward3, 0)
    all_parts(phase3, 1)
    near_units(0)
    arrived("2fwd", 3, {0: one(0)})
    arrived(("3far", -1), 3, SIXTEENTH)
    all_parts(forward3, -1)
    all_parts(phase3, 2)
    near_units(-1)
    far_units(0)
    arrived(("3far", 1), 3, SIXTEENTH)
    all_parts(forward3, 1)
    near_units(1)
    far_units(-1)
    last_request(blocks(1) + blocks(2))
    arrived(("3far", 2), 3, SIXTEENTH)
    all_parts(forward3, 2)
    near_units(2)
    far_units(1)
    last_request(blocks(3))
    far_units(2)
    last_request(blocks(4))
    taken(send_sem.at[0], 9, {})
    taken(send_sem.at[1], 3, EIGHTH)


def exchange(c_raw, k_turned, rope_cos, rope_sin, gain, seq_lens, q_lat, q_rope):
    def shaped(sizes):
        return pltpu.VMEM(tuple(sizes.get(d, FULL[d]) for d in range(6)), BF16)

    hop1 = [shaped({o[0]: 1, o[1]: 2}) for o in ORDERS for _ in PAIR]
    hop2 = [shaped({o[1]: 1, o[2]: 2}) for o in ORDERS for _ in PAIR]
    hop3 = [shaped({o[2]: 1, 3: 1}) for o in ORDERS for _ in PAIR]
    small = [
        pltpu.VMEM((8, 64, 512), BF16),
        pltpu.VMEM((8, 32), F32),
        pltpu.VMEM((8, 32), F32),
        pltpu.VMEM((LATENT,), BF16),
        pltpu.SMEM((REQ,), jnp.int32),
        pltpu.VMEM((4, 16, 512), BF16),
        pltpu.VMEM((4, 16, 64), BF16),
        pltpu.VMEM((4, 128, 512), BF16),
        pltpu.VMEM((128, 256), BF16),
    ]
    sems = [pltpu.SemaphoreType.DMA((n,)) for n in (LOADS, 2, GROUPS)]
    return pl.pallas_call(
        exchange_kernel,
        out_shape=[
            pltpu.VMEM((4, 4, 4, 4, 2, 8, 512), BF16),
            pltpu.VMEM((4, 64, 1024), BF16),
            pltpu.VMEM((SCORE_PARTS,) + FULL[:COL] + (LANES,), F32),
            pltpu.VMEM((8, LANES), jnp.int32),
        ],
        in_specs=[pl.BlockSpec(memory_space=pltpu.HBM)] * 8,
        out_specs=[pl.BlockSpec(memory_space=pltpu.VMEM)] * 4,
        scratch_shapes=[[pltpu.VMEM((9,) + FULL, BF16), shaped({COL: KEY_COLS}), hop1, hop2, hop3, small, sems]],
        compiler_params=pltpu.CompilerParams(collective_id=0, has_side_effects=True, vmem_limit_bytes=40 * 1024 * 1024),
        name="exchange",
    )(c_raw, k_turned, rope_cos, rope_sin, gain, seq_lens, q_lat, q_rope)


def attend_kernel(c_ref, kr_ref, score_ref, len_ref, c_out, kr_out, o_out, o_buf, sem):
    writes = [pltpu.make_async_copy(c_ref, c_out, sem.at[0]), pltpu.make_async_copy(kr_ref, kr_out, sem.at[1])]
    for write in writes:
        write.start()
    row = lax.broadcasted_iota(jnp.int32, (POSITIONS, LANES), 0)
    scores = jnp.where(row < len_ref[0:1, :], jnp.sum(score_ref[...], axis=0) * ATTN_SCALE, -1e30)
    weights = jnp.exp(scores - jnp.max(scores, axis=0, keepdims=True)).T
    weight_sum = jnp.sum(weights[: 4 * HEADS], axis=1, keepdims=True)
    rounded = weights[: 4 * HEADS].astype(BF16)
    for j in REQUESTS:
        mine = slice(HEADS * j, HEADS * (j + 1))
        weighted = jnp.dot(rounded[mine], c_ref[j], preferred_element_type=F32)
        o_buf[j] = (weighted / weight_sum[mine]).astype(BF16)
        writes.append(pltpu.make_async_copy(o_buf.at[j], o_out.at[j], sem.at[2 + j]))
        writes[-1].start()
    for write in writes:
        write.wait()


def attend(c_cache, kr_turned, scores, lens):
    whole = pl.BlockSpec(memory_space=pltpu.VMEM)
    return pl.pallas_call(
        attend_kernel,
        out_shape=[
            jax.ShapeDtypeStruct(c_cache.shape, BF16),
            jax.ShapeDtypeStruct(kr_turned.shape, BF16),
            jax.ShapeDtypeStruct((4, HEADS, LATENT), BF16),
        ],
        in_specs=[whole] * 4,
        out_specs=[pl.BlockSpec(memory_space=pltpu.HBM)] * 3,
        scratch_shapes=[pltpu.VMEM((4, HEADS, LATENT), BF16), pltpu.SemaphoreType.DMA((6,))],
        compiler_params=pltpu.CompilerParams(vmem_limit_bytes=24 * 1024 * 1024),
        name="attend",
    )(c_cache, kr_turned, scores, lens)


def solution(mesh):
    seq_spec = P("dp", "x", None)
    req_spec = P(("dp", "x"), None, None)

    def local_step(c_raw, k_raw, norm_gain, rope_cos, rope_sin, seq_lens, q_lat, q_rope):
        args = (c_raw.reshape(FULL[:4] + (4, 8, LATENT)), k_raw.transpose(1, 2, 0), rope_cos, rope_sin, norm_gain, seq_lens, q_lat, q_rope)
        c_cache, kr_turned, scores, lens = exchange(*[pltpu.with_memory_space_constraint(arg, pltpu.HBM) for arg in args])
        c_cache, kr_turned, o_lat = attend(c_cache.reshape(4, POSITIONS, LATENT), kr_turned, scores.reshape(SCORE_PARTS, POSITIONS, LANES), lens)
        return c_cache, kr_turned.transpose(0, 2, 1), o_lat

    return jax.shard_map(local_step, mesh=mesh, in_specs=(seq_spec, seq_spec, P(None), P("x", None), P("x", None), P("dp"), req_spec, req_spec), out_specs=(req_spec, req_spec, req_spec), check_vma=False)
```

time: 66.5 us -> 64 us (0.962)
  Pallas kernels: 65.1 us -> 62.7 us
    pallas_call x1, Pallas kernels: 61.9 us -> 60.5 us  [exchange(): pl.pallas_call(exchange_kernel, out_shape=[pltpu.VMEM((4, 4, 4, 4, 2, 8,...]
    pallas_call x1, Pallas kernels: 3.17 us -> 2.24 us  [attend(): pl.pallas_call(attend_kernel, out_shape=[jax.ShapeDtypeStruct(c_cache.sha...]
where the time goes in v4:
time: 64 us; the launch traced here: 63.3 us
  Pallas kernels  62.7 us (98%)
  between operations  0.64 us (1%)
    pallas_call x1, Pallas kernels, exchange(): pl.pallas_call(exchange_kernel, out_shape=[pltpu.VMEM((4, 4, 4, 4, 2, 8,...  60.5 us
    pallas_call x1, Pallas kernels, attend(): pl.pallas_call(attend_kernel, out_shape=[jax.ShapeDtypeStruct(c_cache.sha...  2.24 us

profile of v4, /device:TPU:1, one launch (start us, length us, event | category | flops | bytes accessed | tf_op | source)
XLA Modules:
  0.0 63.3 jit_solution(577998403986547928)
XLA Ops:
  0.6 60.5 %exchange.1 = (bf16[4,4,4,4,2,8,512]{6,5,4,3,2,1,0:T(8,128)(2,1)S(1)}, bf16[4,64,1024]{2,1,0:T(8,128)(2,1)S(1)}, f32[5,4,4,4,2,8,128]{6,5,4,3,2,1,0:T(8,128)S(1)}, s32[8,128]{1,0:T(8,128)S(1)}) custom-call(bf16[4,4,4,2,4,8,512]{6,5,4,3,2,1,0:T(8,128)(2,1)} %bitcast.7, bf16[8,64,512]{2,1,0:T(8,128)(2,1)} %bitcast.8, f32[8,32]{1,0:T(8,128)} %cos_ref.1, ...), custom_call_target="tpu_custom_call" | custom-call | tf_op jit(solution)/shard_map/exchange/pallas_call | solution.py:360
  61.1 2.2 %attend.1 = (bf16[4,1024,512]{2,1,0:T(8,128)(2,1)}, bf16[4,64,1024]{2,1,0:T(8,128)(2,1)}, bf16[4,16,512]{2,1,0:T(8,128)(2,1)}) custom-call(bf16[4,1024,512]{2,1,0:T(8,128)(2,1)S(1)} %bitcast.5, bf16[4,64,1024]{2,1,0:T(8,128)(2,1)S(1)} %get-tuple-element.11.kr_ref, f32[5,1024,128]{2,1,0:T(8,128)S(1)} %bitcast.6, s32[8,128]{1,0:T(8,128)S(1)} %get-tuple-element.13.len_ref), custom_call_target="tpu_custom_call" | custom-call | tf_op jit(solution)/shard_map/attend/pallas_call | solution.py:397

commit v5 on v4

--- a/solution.py
+++ b/solution.py
@@ -21,7 +21,6 @@
 REQ = 512
 GROUPS = 23
 LOADS = 9
-SCORE_PARTS = 5
 SIGNS = (1, -1)
 OFFSETS = (0, -1, 1, 2)
 NT = (((1,), (1,)), ((), ()))
@@ -31,7 +30,7 @@
 def exchange_kernel(c_ref, k_ref, cos_ref, sin_ref, gain_ref, len_ref, qlat_ref, qrope_ref, c_out, kr_out, score_out, len_out, scratch):
     parts, k_laid, hop1, hop2, hop3, small, sems = scratch
     mid1, mid2, got = [[parts.at[3 * stage + p] for p in PARTS] for stage in PARTS]
-    k_buf, cos_buf, sin_buf, gain_buf, len_buf, qlat_buf, qrope_buf, q_rows, qk_rows = small
+    k_buf, cos_buf, sin_buf, gain_buf, len_buf, qlat_buf, qrope_buf, q_cols, qk_cols = small
     load_sem, send_sem, recv_sem = sems
 
     me = lax.axis_index("x")
@@ -191,13 +190,13 @@
         mid1[2][index({**own, COL: K_COLS})] = k_laid[index(own)]
 
     def queries():
-        q_rows[...] = jnp.zeros_like(q_rows)
         for j in REQUESTS:
-            q_rows[j, HEADS * j : HEADS * (j + 1), :] = qlat_buf[j]
-        zero = jnp.zeros((HEADS, ROPE), BF16)
-        qk_rows[...] = jnp.zeros_like(qk_rows)
-        for j in REQUESTS:
-            qk_rows[HEADS * j : HEADS * (j + 1), :] = jnp.concatenate([qrope_buf[j] if i == j else zero for i in REQUESTS], axis=1)
+            rows = [qlat_buf[j].astype(F32) if i == j else jnp.zeros((HEADS, LATENT), F32) for i in REQUESTS]
+            q_cols[j] = jnp.concatenate(rows + [jnp.zeros((LANES - 4 * HEADS, LATENT), F32)], axis=0).T.astype(BF16)
+        zero = jnp.zeros((HEADS, ROPE), F32)
+        rows = [jnp.concatenate([qrope_buf[j].astype(F32) if i == j else zero for i in REQUESTS], axis=1) for j in REQUESTS]
+        qk_cols[...] = jnp.concatenate(rows + [jnp.zeros((LANES - 4 * HEADS, KEY_COLS), F32)], axis=0).T.astype(BF16)
+        score_out[...] = jnp.zeros_like(score_out)
         lane = lax.broadcasted_iota(jnp.int32, (8, LANES), 1)
         lens = jnp.zeros((8, LANES), jnp.int32)
         for j in REQUESTS:
@@ -211,40 +210,43 @@
     def unit_shape(a, width):
         return tuple(4 if d == a else 1 for d in range(3)) + (2, 8, width)
 
-    def finish_rows(j, raw, gain, positions, a, where):
-        square = jnp.sum(raw * raw, axis=-1, keepdims=True) * (1.0 / 512)
-        inv_rms = jnp.where(positions < length(j), lax.rsqrt(square + NORM_EPS), 0.0)
-        c_norm = raw * inv_rms * gain
-        c_out[(j,) + where] = c_norm.reshape(unit_shape(a, LATENT)).astype(BF16)
-        part = lax.dot_general(c_norm.astype(BF16), q_rows[j], NT, preferred_element_type=F32)
-        score_out[(j,) + where] = part.reshape(unit_shape(a, LANES))
+    def add_scores(a, wheres, rows, columns):
+        part = jnp.dot(jnp.concatenate(rows, axis=0), columns, preferred_element_type=F32)
+        for i, where in enumerate(wheres):
+            score_out[where] += part[ROWS * i : ROWS * (i + 1)].reshape(unit_shape(a, LANES))
+
+    def finish(j, a, wheres, raws, positions):
+        gain = gain_row()
+        rows = []
+        for where, raw, pos in zip(wheres, raws, positions):
+            square = jnp.sum(raw * raw, axis=-1, keepdims=True) * (1.0 / LATENT)
+            inv_rms = jnp.where(pos < length(j), lax.rsqrt(square + NORM_EPS), 0.0)
+            c_norm = raw * inv_rms * gain
+            c_out[(j,) + where] = c_norm.reshape(unit_shape(a, LATENT)).astype(BF16)
+            rows.append(c_norm.astype(BF16))
+        add_scores(a, wheres, rows, q_cols[j])
 
     def gain_row():
         return gain_buf[...].astype(F32).reshape(1, LATENT)
 
-    def unit(p, ib, ic):
+    def units(p, off, steps):
         a, b, c = ORDERS[p]
-        where = index({b: one(ib), c: one(ic)})[:COL]
-        gain = gain_row()
-        raw = got[p][where + (pl.ds(*C_COLS),)].astype(F32).reshape(ROWS, LATENT)
-        finish_rows(p, raw, gain, row_positions(a, b, c, ib, ic), a, where + (slice(None),))
+        ib, ics = at(b, off), [at(c, step) for step in steps]
+        wheres = [index({b: one(ib), c: one(ic)})[:COL] for ic in ics]
+        full = [where + (slice(None),) for where in wheres]
+        raws = [got[p][where + (pl.ds(*C_COLS),)].astype(F32).reshape(ROWS, LATENT) for where in wheres]
+        finish(p, a, full, raws, [row_positions(a, b, c, ib, ic) for ic in ics])
         if p == 2:
-            tile = got[2][where + (pl.ds(*K_COLS),)].astype(F32).reshape(ROWS, KEY_COLS).astype(BF16)
-            part = lax.dot_general(tile, qk_rows[...], NT, preferred_element_type=F32)
-            score_out[(4,) + where + (slice(None),)] = part.reshape(unit_shape(a, LANES))
+            tiles = [got[2][where + (pl.ds(*K_COLS),)].astype(F32).reshape(ROWS, KEY_COLS).astype(BF16) for where in wheres]
+            add_scores(a, full, tiles, qk_cols[...])
 
     def near_units(off):
         arrived(("3near", off), 5, {0: (0, 3), 1: one(0), CORE: one(0)})
-        for p in PARTS:
-            _, b, c = ORDERS[p]
-            for step in OFFSETS[:3]:
-                unit(p, at(b, off), at(c, step))
+        all_parts(units, off, OFFSETS[:3])
 
     def far_units(off):
         arrived(("3fwd", off), 3, {0: one(0), 1: one(0)})
-        for p in PARTS:
-            _, b, c = ORDERS[p]
-            unit(p, at(b, off), at(c, 2))
+        all_parts(units, off, OFFSETS[3:])
         key_columns(at(ORDERS[2][1], off))
 
     def key_columns(z):
@@ -257,17 +259,11 @@
             valid = col[:ROPE] + z * KEY_COLS < length(j)
             kr_out[j, :, pl.ds(pl.multiple_of(z * KEY_COLS, KEY_COLS), KEY_COLS)] = jnp.where(valid, turned[ROPE * j : ROPE * (j + 1)], 0.0).astype(BF16)
 
-    def last_request(blocks):
-        for off_y, off_x in blocks:
-            y, x = at(1, off_y), at(2, off_x)
-            where = index({1: one(y), 2: one(x)})[:COL]
-            gain = gain_row()
-            raw = [got[p][where + (pl.ds(*K_COLS),)].astype(F32).reshape(ROWS, KEY_COLS) for p in PAIR]
-            finish_rows(3, jnp.concatenate(raw, axis=1), gain, row_positions(0, 1, 2, y, x), 0, where + (slice(None),))
-
-    def blocks(n):
-        inner = OFFSETS[: n - 1]
-        return [(y, x) for y in OFFSETS[:n] for x in OFFSETS[:n] if y not in inner or x not in inner]
+    def last_request(steps):
+        places = [(at(1, y), at(2, x)) for y, x in steps]
+        wheres = [index({1: one(y), 2: one(x)})[:COL] for y, x in places]
+        raws = [jnp.concatenate([got[p][where + (pl.ds(*K_COLS),)].astype(F32).reshape(ROWS, KEY_COLS) for p in PAIR], axis=1) for where in wheres]
+        finish(3, 0, [where + (slice(None),) for where in wheres], raws, [row_positions(0, 1, 2, y, x) for y, x in places])
 
     def all_parts(step, *args):
         for p in PARTS:
@@ -326,14 +322,14 @@
     all_parts(forward3, 1)
     near_units(1)
     far_units(-1)
-    last_request(blocks(1) + blocks(2))
+    last_request([(y, x) for y in OFFSETS[:2] for x in OFFSETS[:2]])
     arrived(("3far", 2), 3, SIXTEENTH)
     all_parts(forward3, 2)
     near_units(2)
     far_units(1)
-    last_request(blocks(3))
+    last_request([(y, x) for y in OFFSETS for x in OFFSETS[:3] if y > 0 or x > 0])
     far_units(2)
-    last_request(blocks(4))
+    last_request([(y, 2) for y in OFFSETS])
     taken(send_sem.at[0], 9, {})
     taken(send_sem.at[1], 3, EIGHTH)
 
@@ -353,8 +349,8 @@
         pltpu.SMEM((REQ,), jnp.int32),
         pltpu.VMEM((4, 16, 512), BF16),
         pltpu.VMEM((4, 16, 64), BF16),
-        pltpu.VMEM((4, 128, 512), BF16),
-        pltpu.VMEM((128, 256), BF16),
+        pltpu.VMEM((4, LATENT, LANES), BF16),
+        pltpu.VMEM((KEY_COLS, LANES), BF16),
     ]
     sems = [pltpu.SemaphoreType.DMA((n,)) for n in (LOADS, 2, GROUPS)]
     return pl.pallas_call(
@@ -362,7 +358,7 @@
         out_shape=[
             pltpu.VMEM((4, 4, 4, 4, 2, 8, 512), BF16),
             pltpu.VMEM((4, 64, 1024), BF16),
-            pltpu.VMEM((SCORE_PARTS,) + FULL[:COL] + (LANES,), F32),
+            pltpu.VMEM(FULL[:COL] + (LANES,), F32),
             pltpu.VMEM((8, LANES), jnp.int32),
         ],
         in_specs=[pl.BlockSpec(memory_space=pltpu.HBM)] * 8,
@@ -374,11 +370,19 @@
 
 
 def attend_kernel(c_ref, kr_ref, score_ref, len_ref, c_out, kr_out, o_out, o_buf, sem):
-    writes = [pltpu.make_async_copy(c_ref, c_out, sem.at[0]), pltpu.make_async_copy(kr_ref, kr_out, sem.at[1])]
-    for write in writes:
-        write.start()
+    writes = []
+
+    def write(a, b):
+        writes.append(pltpu.make_async_copy(a, b, sem.at[len(writes)]))
+        writes[-1].start()
+
+    for j in REQUESTS:
+        for half in PAIR:
+            rows = pl.ds(half * (POSITIONS // 2), POSITIONS // 2)
+            write(c_ref.at[j, rows], c_out.at[j, rows])
+    write(kr_ref, kr_out)
     row = lax.broadcasted_iota(jnp.int32, (POSITIONS, LANES), 0)
-    scores = jnp.where(row < len_ref[0:1, :], jnp.sum(score_ref[...], axis=0) * ATTN_SCALE, -1e30)
+    scores = jnp.where(row < len_ref[0:1, :], score_ref[...] * ATTN_SCALE, -1e30)
     weights = jnp.exp(scores - jnp.max(scores, axis=0, keepdims=True)).T
     weight_sum = jnp.sum(weights[: 4 * HEADS], axis=1, keepdims=True)
     rounded = weights[: 4 * HEADS].astype(BF16)
@@ -386,10 +390,9 @@
         mine = slice(HEADS * j, HEADS * (j + 1))
         weighted = jnp.dot(rounded[mine], c_ref[j], preferred_element_type=F32)
         o_buf[j] = (weighted / weight_sum[mine]).astype(BF16)
-        writes.append(pltpu.make_async_copy(o_buf.at[j], o_out.at[j], sem.at[2 + j]))
-        writes[-1].start()
-    for write in writes:
-        write.wait()
+        write(o_buf.at[j], o_out.at[j])
+    for copy in writes:
+        copy.wait()
 
 
 def attend(c_cache, kr_turned, scores, lens):
@@ -403,7 +406,7 @@
         ],
         in_specs=[whole] * 4,
         out_specs=[pl.BlockSpec(memory_space=pltpu.HBM)] * 3,
-        scratch_shapes=[pltpu.VMEM((4, HEADS, LATENT), BF16), pltpu.SemaphoreType.DMA((6,))],
+        scratch_shapes=[pltpu.VMEM((4, HEADS, LATENT), BF16), pltpu.SemaphoreType.DMA((13,))],
         compiler_params=pltpu.CompilerParams(vmem_limit_bytes=24 * 1024 * 1024),
         name="attend",
     )(c_cache, kr_turned, scores, lens)
@@ -416,7 +419,7 @@
     def local_step(c_raw, k_raw, norm_gain, rope_cos, rope_sin, seq_lens, q_lat, q_rope):
         args = (c_raw.reshape(FULL[:4] + (4, 8, LATENT)), k_raw.transpose(1, 2, 0), rope_cos, rope_sin, norm_gain, seq_lens, q_lat, q_rope)
         c_cache, kr_turned, scores, lens = exchange(*[pltpu.with_memory_space_constraint(arg, pltpu.HBM) for arg in args])
-        c_cache, kr_turned, o_lat = attend(c_cache.reshape(4, POSITIONS, LATENT), kr_turned, scores.reshape(SCORE_PARTS, POSITIONS, LANES), lens)
+        c_cache, kr_turned, o_lat = attend(c_cache.reshape(4, POSITIONS, LATENT), kr_turned, scores.reshape(POSITIONS, LANES), lens)
         return c_cache, kr_turned.transpose(0, 2, 1), o_lat
 
     return jax.shard_map(local_step, mesh=mesh, in_specs=(seq_spec, seq_spec, P(None), P("x", None), P("x", None), P("dp"), req_spec, req_spec), out_specs=(req_spec, req_spec, req_spec), check_vma=False)

time: 64 us -> 63.8 us (level)
  no operation moved by 1% of the time
where the time goes in v5:
time: 63.8 us; the launch traced here: 63.1 us
  Pallas kernels  62.5 us (98%)
  between operations  0.64 us (1%)
    pallas_call x1, Pallas kernels, exchange(): pl.pallas_call(exchange_kernel, out_shape=[pltpu.VMEM((4, 4, 4, 4, 2, 8,...  60.2 us
    pallas_call x1, Pallas kernels, attend(): pl.pallas_call(attend_kernel, out_shape=[jax.ShapeDtypeStruct(c_cache.sha...  2.3 us

profile of v5, /device:TPU:1, one launch (start us, length us, event | category | flops | bytes accessed | tf_op | source)
XLA Modules:
  0.0 63.1 jit_solution(69246877546260053)
XLA Ops:
  0.6 60.2 %exchange.1 = (bf16[4,4,4,4,2,8,512]{6,5,4,3,2,1,0:T(8,128)(2,1)S(1)}, bf16[4,64,1024]{2,1,0:T(8,128)(2,1)S(1)}, f32[4,4,4,2,8,128]{5,4,3,2,1,0:T(8,128)S(1)}, s32[8,128]{1,0:T(8,128)S(1)}) custom-call(bf16[4,4,4,2,4,8,512]{6,5,4,3,2,1,0:T(8,128)(2,1)} %bitcast.7, bf16[8,64,512]{2,1,0:T(8,128)(2,1)} %bitcast.8, f32[8,32]{1,0:T(8,128)} %cos_ref.1, ...), custom_call_target="tpu_custom_call" | custom-call | tf_op jit(solution)/shard_map/exchange/pallas_call | solution.py:356
  60.8 2.3 %attend.1 = (bf16[4,1024,512]{2,1,0:T(8,128)(2,1)}, bf16[4,64,1024]{2,1,0:T(8,128)(2,1)}, bf16[4,16,512]{2,1,0:T(8,128)(2,1)}) custom-call(bf16[4,1024,512]{2,1,0:T(8,128)(2,1)S(1)} %bitcast.5, bf16[4,64,1024]{2,1,0:T(8,128)(2,1)S(1)} %get-tuple-element.11.kr_ref, f32[1024,128]{1,0:T(8,128)S(1)} %bitcast.6, s32[8,128]{1,0:T(8,128)S(1)} %get-tuple-element.13.len_ref), custom_call_target="tpu_custom_call" | custom-call | tf_op jit(solution)/shard_map/attend/pallas_call | solution.py:400

commit v6 on v5

--- a/solution.py
+++ b/solution.py
@@ -20,7 +20,7 @@
 REQUESTS = range(4)
 REQ = 512
 GROUPS = 23
-LOADS = 9
+LOADS = 11
 SIGNS = (1, -1)
 OFFSETS = (0, -1, 1, 2)
 NT = (((1,), (1,)), ((), ()))
@@ -28,7 +28,7 @@
 
 
 def exchange_kernel(c_ref, k_ref, cos_ref, sin_ref, gain_ref, len_ref, qlat_ref, qrope_ref, c_out, kr_out, score_out, len_out, scratch):
-    parts, k_laid, hop1, hop2, hop3, small, sems = scratch
+    parts, k_laid, staged, hop1, hop2, hop3, small, sems = scratch
     mid1, mid2, got = [[parts.at[3 * stage + p] for p in PARTS] for stage in PARTS]
     k_buf, cos_buf, sin_buf, gain_buf, len_buf, qlat_buf, qrope_buf, q_cols, qk_cols = small
     load_sem, send_sem, recv_sem = sems
@@ -82,6 +82,12 @@
         copy.start()
         return copy
 
+    for extra in (False, True):
+        for p in PARTS[: 2 if extra else 3]:
+            a, b, _ = ORDERS[p]
+            for s in PAIR:
+                far = {a: one(at(a, 2)), b: halves(s)}
+                load(8 if p == 2 else 7, taken_from(p, far, extra), view(staged[2 * p + s], {COL: K_COLS if extra else C_COLS}))
     key_loads = [load(i, a, b) for i, (a, b) in enumerate(((k_ref, k_buf), (cos_ref, cos_buf), (sin_ref, sin_buf)))]
     other_loads = [load(3 + i, a, b) for i, (a, b) in enumerate(((gain_ref, gain_buf), (len_ref, len_buf), (qlat_ref, qlat_buf), (qrope_ref, qrope_buf)))]
     for p in PARTS:
@@ -111,7 +117,8 @@
         a, b, _ = ORDERS[p]
         wide = {COL: cols}
         for s, sign in enumerate(SIGNS):
-            send(first_group(p, cols), held(p, {a: one(at(a, 2)), b: halves(s)}, cols), view(hop1[2 * p + s], wide), device(a, sign))
+            source = view(k_laid, {a: one(at(a, 2)), b: halves(s)}) if cols == K_COLS else view(staged[2 * p + s], wide)
+            send(first_group(p, cols), source, view(hop1[2 * p + s], wide), device(a, sign))
 
     def near1(p, cols):
         a, b, _ = ORDERS[p]
@@ -271,10 +278,14 @@
 
     EIGHTH, SIXTEENTH = {0: one(0), 1: (0, 2)}, {0: one(0), 1: one(0)}
     pl.semaphore_wait(barrier, 13)
-    for first in (far1, near1):
-        all_parts(first, C_COLS)
-        first(0, K_COLS)
-        first(1, K_COLS)
+    taken(load_sem.at[7], 2, {0: one(0)})
+    far1(0, ALL_COLS)
+    far1(1, ALL_COLS)
+    taken(load_sem.at[8], 1, {0: one(0), COL: C_COLS})
+    far1(2, C_COLS)
+    all_parts(near1, C_COLS)
+    near1(0, K_COLS)
+    near1(1, K_COLS)
     for copy in key_loads:
         copy.wait()
     keys()
@@ -363,7 +374,7 @@
         ],
         in_specs=[pl.BlockSpec(memory_space=pltpu.HBM)] * 8,
         out_specs=[pl.BlockSpec(memory_space=pltpu.VMEM)] * 4,
-        scratch_shapes=[[pltpu.VMEM((9,) + FULL, BF16), shaped({COL: KEY_COLS}), hop1, hop2, hop3, small, sems]],
+        scratch_shapes=[[pltpu.VMEM((9,) + FULL, BF16), shaped({COL: KEY_COLS}), hop1, hop1, hop2, hop3, small, sems]],
         compiler_params=pltpu.CompilerParams(collective_id=0, has_side_effects=True, vmem_limit_bytes=40 * 1024 * 1024),
         name="exchange",
     )(c_raw, k_turned, rope_cos, rope_sin, gain, seq_lens, q_lat, q_rope)

time: 63.8 us -> 63.9 us (level)
  no operation moved by 1% of the time
where the time goes in v6:
time: 63.9 us; the launch traced here: 63.1 us
  Pallas kernels  62.5 us (98%)
  between operations  0.64 us (1%)
    pallas_call x1, Pallas kernels, exchange(): pl.pallas_call(exchange_kernel, out_shape=[pltpu.VMEM((4, 4, 4, 4, 2, 8,...  60.2 us
    pallas_call x1, Pallas kernels, attend(): pl.pallas_call(attend_kernel, out_shape=[jax.ShapeDtypeStruct(c_cache.sha...  2.3 us

profile of v6, /device:TPU:1, one launch (start us, length us, event | category | flops | bytes accessed | tf_op | source)
XLA Modules:
  0.0 63.1 jit_solution(15060631364268923641)
XLA Ops:
  0.6 60.2 %exchange.1 = (bf16[4,4,4,4,2,8,512]{6,5,4,3,2,1,0:T(8,128)(2,1)S(1)}, bf16[4,64,1024]{2,1,0:T(8,128)(2,1)S(1)}, f32[4,4,4,2,8,128]{5,4,3,2,1,0:T(8,128)S(1)}, s32[8,128]{1,0:T(8,128)S(1)}) custom-call(bf16[4,4,4,2,4,8,512]{6,5,4,3,2,1,0:T(8,128)(2,1)} %bitcast.7, bf16[8,64,512]{2,1,0:T(8,128)(2,1)} %bitcast.8, f32[8,32]{1,0:T(8,128)} %cos_ref.1, ...), custom_call_target="tpu_custom_call" | custom-call | tf_op jit(solution)/shard_map/exchange/pallas_call | solution.py:367
  60.8 2.3 %attend.1 = (bf16[4,1024,512]{2,1,0:T(8,128)(2,1)}, bf16[4,64,1024]{2,1,0:T(8,128)(2,1)}, bf16[4,16,512]{2,1,0:T(8,128)(2,1)}) custom-call(bf16[4,1024,512]{2,1,0:T(8,128)(2,1)S(1)} %bitcast.5, bf16[4,64,1024]{2,1,0:T(8,128)(2,1)S(1)} %get-tuple-element.11.kr_ref, f32[1024,128]{1,0:T(8,128)S(1)} %bitcast.6, s32[8,128]{1,0:T(8,128)S(1)} %get-tuple-element.13.len_ref), custom_call_target="tpu_custom_call" | custom-call | tf_op jit(solution)/shard_map/attend/pallas_call | solution.py:411

commit v7 on v5

--- a/solution.py
+++ b/solution.py
@@ -27,32 +27,100 @@
 F32, BF16 = jnp.float32, jnp.bfloat16
 
 
-def exchange_kernel(c_ref, k_ref, cos_ref, sin_ref, gain_ref, len_ref, qlat_ref, qrope_ref, c_out, kr_out, score_out, len_out, scratch):
+def all_parts(step, *args):
+    for p in PARTS:
+        step(p, *args)
+
+
+def index(sel, dims=len(FULL)):
+    return tuple(pl.ds(*sel[d]) if d in sel else slice(None) for d in range(dims))
+
+
+def one(i):
+    return (i, 1)
+
+
+def place_of(me):
+    return (me // 32, (me // 8) % 4, (me // 2) % 4)
+
+
+def stepper(place):
+    return lambda dim, delta: (place[dim] + delta + 4) % 4
+
+
+def row_work(at, length, got, gain_row, q_cols, qk_cols, c_out, kr_out, score_out):
+    def row_positions(a, b, c, ib, ic):
+        r = lax.broadcasted_iota(jnp.int32, (ROWS, 1), 0)
+        return (r // 16) * STRIDES[a] + r % 16 + ib * STRIDES[b] + ic * STRIDES[c]
+
+    def unit_shape(a, width):
+        return tuple(4 if d == a else 1 for d in range(3)) + (2, 8, width)
+
+    def add_scores(a, wheres, rows, columns):
+        part = jnp.dot(jnp.concatenate(rows, axis=0), columns, preferred_element_type=F32)
+        for i, where in enumerate(wheres):
+            score_out[where] += part[ROWS * i : ROWS * (i + 1)].reshape(unit_shape(a, LANES))
+
+    def finish(j, a, wheres, raws, positions):
+        gain = gain_row()
+        rows = []
+        for where, raw, pos in zip(wheres, raws, positions):
+            square = jnp.sum(raw * raw, axis=-1, keepdims=True) * (1.0 / LATENT)
+            inv_rms = jnp.where(pos < length(j), lax.rsqrt(square + NORM_EPS), 0.0)
+            c_norm = raw * inv_rms * gain
+            c_out[(j,) + where] = c_norm.reshape(unit_shape(a, LATENT)).astype(BF16)
+            rows.append(c_norm.astype(BF16))
+        add_scores(a, wheres, rows, q_cols[j])
+
+    def units(p, off, steps):
+        a, b, c = ORDERS[p]
+        ib, ics = at(b, off), [at(c, step) for step in steps]
+        wheres = [index({b: one(ib), c: one(ic)})[:COL] for ic in ics]
+        full = [where + (slice(None),) for where in wheres]
+        raws = [got[p][where + (pl.ds(*C_COLS),)].astype(F32).reshape(ROWS, LATENT) for where in wheres]
+        finish(p, a, full, raws, [row_positions(a, b, c, ib, ic) for ic in ics])
+        if p == 2:
+            tiles = [got[2][where + (pl.ds(*K_COLS),)].astype(F32).reshape(ROWS, KEY_COLS).astype(BF16) for where in wheres]
+            add_scores(a, full, tiles, qk_cols[...])
+
+    def key_columns(z):
+        row = lax.broadcasted_iota(jnp.int32, (KEY_COLS, KEY_COLS), 0)
+        col = lax.broadcasted_iota(jnp.int32, (KEY_COLS, KEY_COLS), 1)
+        eye = jnp.where(row == col, 1.0, 0.0).astype(BF16)
+        tile = got[2][pl.ds(z, 1), :, :, :, :, pl.ds(*K_COLS)].astype(F32).reshape(KEY_COLS, KEY_COLS).astype(BF16)
+        turned = lax.dot_general(eye, tile, NT, preferred_element_type=F32)
+        for j in REQUESTS:
+            valid = col[:ROPE] + z * KEY_COLS < length(j)
+            kr_out[j, :, pl.ds(pl.multiple_of(z * KEY_COLS, KEY_COLS), KEY_COLS)] = jnp.where(valid, turned[ROPE * j : ROPE * (j + 1)], 0.0).astype(BF16)
+
+    def last_request(steps):
+        places = [(at(1, y), at(2, x)) for y, x in steps]
+        wheres = [index({1: one(y), 2: one(x)})[:COL] for y, x in places]
+        raws = [jnp.concatenate([got[p][where + (pl.ds(*K_COLS),)].astype(F32).reshape(ROWS, KEY_COLS) for p in PAIR], axis=1) for where in wheres]
+        finish(3, 0, [where + (slice(None),) for where in wheres], raws, [row_positions(0, 1, 2, y, x) for y, x in places])
+
+    return units, last_request, key_columns
+
+
+def exchange_kernel(c_ref, k_ref, cos_ref, sin_ref, gain_ref, len_ref, qlat_ref, qrope_ref, c_out, kr_out, score_out, len_out, got, q_cols, qk_cols, gain_out, scratch):
     parts, k_laid, hop1, hop2, hop3, small, sems = scratch
-    mid1, mid2, got = [[parts.at[3 * stage + p] for p in PARTS] for stage in PARTS]
-    k_buf, cos_buf, sin_buf, gain_buf, len_buf, qlat_buf, qrope_buf, q_cols, qk_cols = small
+    mid1, mid2 = [[parts.at[3 * stage + p] for p in PARTS] for stage in PAIR]
+    got = [got.at[p] for p in PARTS]
+    k_buf, cos_buf, sin_buf, gain_buf, len_buf, qlat_buf, qrope_buf = small
     load_sem, send_sem, recv_sem = sems
 
     me = lax.axis_index("x")
     core = me % 2
     other = me + 1 - 2 * core
     cores = (core, 1 - core)
-    place = (me // 32, (me // 8) % 4, (me // 2) % 4)
+    place = place_of(me)
+    at = stepper(place)
 
     def device(dim, delta, to_core=None):
         pos = list(place)
         pos[dim] = (pos[dim] + delta + 4) % 4
         last = core if to_core is None else to_core
         return ((pos[0] * 4 + pos[1]) * 4 + pos[2]) * 2 + last
-
-    def at(dim, delta):
-        return (place[dim] + delta + 4) % 4
-
-    def index(sel, dims=len(FULL)):
-        return tuple(pl.ds(*sel[d]) if d in sel else slice(None) for d in range(dims))
-
-    def one(i):
-        return (i, 1)
 
     def halves(s):
         return (2 * s, 2)
@@ -201,44 +269,11 @@
         lens = jnp.zeros((8, LANES), jnp.int32)
         for j in REQUESTS:
             lens = jnp.where(lane // HEADS == j, length(j), lens)
-        len_out[...] = lens
-
-    def row_positions(a, b, c, ib, ic):
-        r = lax.broadcasted_iota(jnp.int32, (ROWS, 1), 0)
-        return (r // 16) * STRIDES[a] + r % 16 + ib * STRIDES[b] + ic * STRIDES[c]
-
-    def unit_shape(a, width):
-        return tuple(4 if d == a else 1 for d in range(3)) + (2, 8, width)
-
-    def add_scores(a, wheres, rows, columns):
-        part = jnp.dot(jnp.concatenate(rows, axis=0), columns, preferred_element_type=F32)
-        for i, where in enumerate(wheres):
-            score_out[where] += part[ROWS * i : ROWS * (i + 1)].reshape(unit_shape(a, LANES))
-
-    def finish(j, a, wheres, raws, positions):
-        gain = gain_row()
-        rows = []
-        for where, raw, pos in zip(wheres, raws, positions):
-            square = jnp.sum(raw * raw, axis=-1, keepdims=True) * (1.0 / LATENT)
-            inv_rms = jnp.where(pos < length(j), lax.rsqrt(square + NORM_EPS), 0.0)
-            c_norm = raw * inv_rms * gain
-            c_out[(j,) + where] = c_norm.reshape(unit_shape(a, LATENT)).astype(BF16)
-            rows.append(c_norm.astype(BF16))
-        add_scores(a, wheres, rows, q_cols[j])
-
-    def gain_row():
-        return gain_buf[...].astype(F32).reshape(1, LATENT)
-
-    def units(p, off, steps):
-        a, b, c = ORDERS[p]
-        ib, ics = at(b, off), [at(c, step) for step in steps]
-        wheres = [index({b: one(ib), c: one(ic)})[:COL] for ic in ics]
-        full = [where + (slice(None),) for where in wheres]
-        raws = [got[p][where + (pl.ds(*C_COLS),)].astype(F32).reshape(ROWS, LATENT) for where in wheres]
-        finish(p, a, full, raws, [row_positions(a, b, c, ib, ic) for ic in ics])
-        if p == 2:
-            tiles = [got[2][where + (pl.ds(*K_COLS),)].astype(F32).reshape(ROWS, KEY_COLS).astype(BF16) for where in wheres]
-            add_scores(a, full, tiles, qk_cols[...])
+            len_out[j] = jnp.zeros((8, LANES), jnp.int32) + length(j)
+        len_out[4] = lens
+        gain_out[...] = jnp.broadcast_to(gain_buf[...].astype(F32).reshape(1, LATENT), gain_out.shape)
+
+    units, last_request, key_columns = row_work(at, length, got, lambda: gain_out[0:1, :], q_cols, qk_cols, c_out, kr_out, score_out)
 
     def near_units(off):
         arrived(("3near", off), 5, {0: (0, 3), 1: one(0), CORE: one(0)})
@@ -248,26 +283,6 @@
         arrived(("3fwd", off), 3, {0: one(0), 1: one(0)})
         all_parts(units, off, OFFSETS[3:])
         key_columns(at(ORDERS[2][1], off))
-
-    def key_columns(z):
-        row = lax.broadcasted_iota(jnp.int32, (KEY_COLS, KEY_COLS), 0)
-        col = lax.broadcasted_iota(jnp.int32, (KEY_COLS, KEY_COLS), 1)
-        eye = jnp.where(row == col, 1.0, 0.0).astype(BF16)
-        tile = got[2][pl.ds(z, 1), :, :, :, :, pl.ds(*K_COLS)].astype(F32).reshape(KEY_COLS, KEY_COLS).astype(BF16)
-        turned = lax.dot_general(eye, tile, NT, preferred_element_type=F32)
-        for j in REQUESTS:
-            valid = col[:ROPE] + z * KEY_COLS < length(j)
-            kr_out[j, :, pl.ds(pl.multiple_of(z * KEY_COLS, KEY_COLS), KEY_COLS)] = jnp.where(valid, turned[ROPE * j : ROPE * (j + 1)], 0.0).astype(BF16)
-
-    def last_request(steps):
-        places = [(at(1, y), at(2, x)) for y, x in steps]
-        wheres = [index({1: one(y), 2: one(x)})[:COL] for y, x in places]
-        raws = [jnp.concatenate([got[p][where + (pl.ds(*K_COLS),)].astype(F32).reshape(ROWS, KEY_COLS) for p in PAIR], axis=1) for where in wheres]
-        finish(3, 0, [where + (slice(None),) for where in wheres], raws, [row_positions(0, 1, 2, y, x) for y, x in places])
-
-    def all_parts(step, *args):
-        for p in PARTS:
-            step(p, *args)
 
     EIGHTH, SIXTEENTH = {0: one(0), 1: (0, 2)}, {0: one(0), 1: one(0)}
     pl.semaphore_wait(barrier, 13)
@@ -328,8 +343,7 @@
     near_units(2)
     far_units(1)
     last_request([(y, x) for y in OFFSETS for x in OFFSETS[:3] if y > 0 or x > 0])
-    far_units(2)
-    last_request([(y, 2) for y in OFFSETS])
+    arrived(("3fwd", 2), 3, SIXTEENTH)
     taken(send_sem.at[0], 9, {})
     taken(send_sem.at[1], 3, EIGHTH)
 
@@ -349,8 +363,6 @@
         pltpu.SMEM((REQ,), jnp.int32),
         pltpu.VMEM((4, 16, 512), BF16),
         pltpu.VMEM((4, 16, 64), BF16),
-        pltpu.VMEM((4, LATENT, LANES), BF16),
-        pltpu.VMEM((KEY_COLS, LANES), BF16),
     ]
     sems = [pltpu.SemaphoreType.DMA((n,)) for n in (LOADS, 2, GROUPS)]
     return pl.pallas_call(
@@ -359,57 +371,90 @@
             pltpu.VMEM((4, 4, 4, 4, 2, 8, 512), BF16),
             pltpu.VMEM((4, 64, 1024), BF16),
             pltpu.VMEM(FULL[:COL] + (LANES,), F32),
-            pltpu.VMEM((8, LANES), jnp.int32),
+            pltpu.VMEM((5, 8, LANES), jnp.int32),
+            pltpu.VMEM((3,) + FULL, BF16),
+            pltpu.VMEM((4, LATENT, LANES), BF16),
+            pltpu.VMEM((KEY_COLS, LANES), BF16),
+            pltpu.VMEM((8, LATENT), F32),
         ],
         in_specs=[pl.BlockSpec(memory_space=pltpu.HBM)] * 8,
-        out_specs=[pl.BlockSpec(memory_space=pltpu.VMEM)] * 4,
+        out_specs=[pl.BlockSpec(memory_space=pltpu.VMEM)] * 8,
         scratch_shapes=[[pltpu.VMEM((9,) + FULL, BF16), shaped({COL: KEY_COLS}), hop1, hop2, hop3, small, sems]],
         compiler_params=pltpu.CompilerParams(collective_id=0, has_side_effects=True, vmem_limit_bytes=40 * 1024 * 1024),
         name="exchange",
     )(c_raw, k_turned, rope_cos, rope_sin, gain, seq_lens, q_lat, q_rope)
 
 
-def attend_kernel(c_ref, kr_ref, score_ref, len_ref, c_out, kr_out, o_out, o_buf, sem):
+def attend_kernel(c_in, kr_in, score_in, len_ref, got_ref, q_cols, qk_cols, gain_ref, c_hbm, kr_hbm, o_hbm, c_buf, kr_buf, scores, o_buf, sem):
+    at = stepper(place_of(lax.axis_index("x")))
     writes = []
 
     def write(a, b):
-        writes.append(pltpu.make_async_copy(a, b, sem.at[len(writes)]))
+        writes.append(pltpu.make_async_copy(a, b, sem))
         writes[-1].start()
 
-    for j in REQUESTS:
-        for half in PAIR:
-            rows = pl.ds(half * (POSITIONS // 2), POSITIONS // 2)
-            write(c_ref.at[j, rows], c_out.at[j, rows])
-    write(kr_ref, kr_out)
+    def write_rows(j, sel):
+        where = (j,) + index(sel)
+        write(c_buf.at[where], c_hbm.at[where])
+
+    def write_keys(z):
+        where = (slice(None), slice(None), pl.ds(pl.multiple_of(z * KEY_COLS, KEY_COLS), KEY_COLS))
+        write(kr_buf.at[where], kr_hbm.at[where])
+
+    near, far = OFFSETS[:3], OFFSETS[3]
+    for p, (_, b, c) in enumerate(ORDERS):
+        for off in near:
+            write_rows(p, {b: one(at(b, off))})
+        for off in near:
+            write_rows(p, {b: one(at(b, far)), c: one(at(c, off))})
+    for off in near:
+        write_rows(3, {2: one(at(2, off))})
+        write_keys(at(ORDERS[2][1], off))
+
+    got = [got_ref.at[p] for p in PARTS]
+    units, last_request, key_columns = row_work(at, lambda j: len_ref[j, 0:1, 0:1], got, lambda: gain_ref[0:1, :], q_cols, qk_cols, c_buf, kr_buf, scores)
+    all_parts(units, far, OFFSETS[3:])
+    last_request([(y, far) for y in OFFSETS])
+    for p, (_, b, c) in enumerate(ORDERS):
+        write_rows(p, {b: one(at(b, far)), c: one(at(c, far))})
+    write_rows(3, {2: one(at(2, far))})
+    key_columns(at(ORDERS[2][1], far))
+    write_keys(at(ORDERS[2][1], far))
+
     row = lax.broadcasted_iota(jnp.int32, (POSITIONS, LANES), 0)
-    scores = jnp.where(row < len_ref[0:1, :], score_ref[...] * ATTN_SCALE, -1e30)
-    weights = jnp.exp(scores - jnp.max(scores, axis=0, keepdims=True)).T
+    masked = jnp.where(row < len_ref[4, 0:1, :], scores[...].reshape(POSITIONS, LANES) * ATTN_SCALE, -1e30)
+    weights = jnp.exp(masked - jnp.max(masked, axis=0, keepdims=True)).T
     weight_sum = jnp.sum(weights[: 4 * HEADS], axis=1, keepdims=True)
     rounded = weights[: 4 * HEADS].astype(BF16)
     for j in REQUESTS:
         mine = slice(HEADS * j, HEADS * (j + 1))
-        weighted = jnp.dot(rounded[mine], c_ref[j], preferred_element_type=F32)
+        weighted = jnp.dot(rounded[mine], c_buf[j].reshape(POSITIONS, LATENT), preferred_element_type=F32)
         o_buf[j] = (weighted / weight_sum[mine]).astype(BF16)
-        write(o_buf.at[j], o_out.at[j])
+        write(o_buf.at[j], o_hbm.at[j])
     for copy in writes:
         copy.wait()
 
 
-def attend(c_cache, kr_turned, scores, lens):
-    whole = pl.BlockSpec(memory_space=pltpu.VMEM)
+def attend(*handed):
+    c_cache, kr_turned, scores = handed[:3]
+    in_hbm, in_vmem = pl.BlockSpec(memory_space=pltpu.HBM), pl.BlockSpec(memory_space=pltpu.VMEM)
     return pl.pallas_call(
         attend_kernel,
         out_shape=[
             jax.ShapeDtypeStruct(c_cache.shape, BF16),
             jax.ShapeDtypeStruct(kr_turned.shape, BF16),
             jax.ShapeDtypeStruct((4, HEADS, LATENT), BF16),
+            pltpu.VMEM(c_cache.shape, BF16),
+            pltpu.VMEM(kr_turned.shape, BF16),
+            pltpu.VMEM(scores.shape, F32),
         ],
-        in_specs=[whole] * 4,
-        out_specs=[pl.BlockSpec(memory_space=pltpu.HBM)] * 3,
-        scratch_shapes=[pltpu.VMEM((4, HEADS, LATENT), BF16), pltpu.SemaphoreType.DMA((13,))],
-        compiler_params=pltpu.CompilerParams(vmem_limit_bytes=24 * 1024 * 1024),
+        in_specs=[in_vmem] * len(handed),
+        out_specs=[in_hbm] * 3 + [in_vmem] * 3,
+        input_output_aliases={0: 3, 1: 4, 2: 5},
+        scratch_shapes=[pltpu.VMEM((4, HEADS, LATENT), BF16), pltpu.SemaphoreType.DMA],
+        compiler_params=pltpu.CompilerParams(vmem_limit_bytes=16 * 1024 * 1024),
         name="attend",
-    )(c_cache, kr_turned, scores, lens)
+    )(*handed)[:3]
 
 
 def solution(mesh):
@@ -418,8 +463,9 @@
 
     def local_step(c_raw, k_raw, norm_gain, rope_cos, rope_sin, seq_lens, q_lat, q_rope):
         args = (c_raw.reshape(FULL[:4] + (4, 8, LATENT)), k_raw.transpose(1, 2, 0), rope_cos, rope_sin, norm_gain, seq_lens, q_lat, q_rope)
-        c_cache, kr_turned, scores, lens = exchange(*[pltpu.with_memory_space_constraint(arg, pltpu.HBM) for arg in args])
-        c_cache, kr_turned, o_lat = attend(c_cache.reshape(4, POSITIONS, LATENT), kr_turned, scores.reshape(POSITIONS, LANES), lens)
+        handed = exchange(*[pltpu.with_memory_space_constraint(arg, pltpu.HBM) for arg in args])
+        c_cache, kr_turned, o_lat = attend(*handed)
+        c_cache = c_cache.reshape(4, POSITIONS, LATENT)
         return c_cache, kr_turned.transpose(0, 2, 1), o_lat
 
     return jax.shard_map(local_step, mesh=mesh, in_specs=(seq_spec, seq_spec, P(None), P("x", None), P("x", None), P("dp"), req_spec, req_spec), out_specs=(req_spec, req_spec, req_spec), check_vma=False)

time: 63.8 us -> 63.3 us (level)
  no operation moved by 1% of the time
where the time goes in v7:
time: 63.3 us; the launch traced here: 62.5 us
  Pallas kernels  61.9 us (98%)
  between operations  0.64 us (1%)
    pallas_call x1, Pallas kernels, exchange(): pl.pallas_call(exchange_kernel, out_shape=[pltpu.VMEM((4, 4, 4, 4, 2, 8,...  59.7 us
    pallas_call x1, Pallas kernels, attend(): pl.pallas_call(attend_kernel, out_shape=[jax.ShapeDtypeStruct(c_cache.sha...  2.21 us

profile of v7, /device:TPU:1, one launch (start us, length us, event | category | flops | bytes accessed | tf_op | source)
XLA Modules:
  0.0 62.5 jit_solution(8069329324748589871)
XLA Ops:
  0.6 59.7 %exchange.1 = (bf16[4,4,4,4,2,8,512]{6,5,4,3,2,1,0:T(8,128)(2,1)S(1)}, bf16[4,64,1024]{2,1,0:T(8,128)(2,1)S(1)}, f32[4,4,4,2,8,128]{5,4,3,2,1,0:T(8,128)S(1)}, s...) custom-call(bf16[4,4,4,2,4,8,512]{6,5,4,3,2,1,0:T(8,128)(2,1)} %bitc, ...), custom_call_target="tpu_custom_call" | custom-call | tf_op jit(solution)/shard_map/exchange/pallas_call | solution.py:368
  60.3 2.2 %attend.1 = (bf16[4,4,4,4,2,8,512]{6,5,4,3,2,1,0:T(8,128)(2,1)}, bf16[4,64,1024]{2,1,0:T(8,128)(2,1)}, bf16[4,16,512]{2,1,0:T(8,128)(2,1)}, bf16[4,4,4,4,2,8,512...) custom-call(bf16[4,4,4,4,2,8,512]{6,5,4,3,2,1,0:T(8,128)(2,1)S(1)} %, ...), custom_call_target="tpu_custom_call", output_to_operand_aliasing={{3}: (0, {}), {4}: (1, {}), {5}: (2, {})} | custom-call | tf_op jit(solution)/shard_map/attend/pallas_call | solution.py:441

commit v8 on v7

--- a/solution.py
+++ b/solution.py
@@ -103,7 +103,7 @@
 
 
 def exchange_kernel(c_ref, k_ref, cos_ref, sin_ref, gain_ref, len_ref, qlat_ref, qrope_ref, c_out, kr_out, score_out, len_out, got, q_cols, qk_cols, gain_out, scratch):
-    parts, k_laid, hop1, hop2, hop3, small, sems = scratch
+    parts, k_laid, hop1, hop2, hop3, hop4, small, sems = scratch
     mid1, mid2 = [[parts.at[3 * stage + p] for p in PARTS] for stage in PAIR]
     got = [got.at[p] for p in PARTS]
     k_buf, cos_buf, sin_buf, gain_buf, len_buf, qlat_buf, qrope_buf = small
@@ -212,23 +212,31 @@
     def phase3(p, off):
         a, b, c = ORDERS[p]
         sb = {b: one(at(b, off))}
-        hop_sb = {b: one(off % 4)}
         got_b = mid1[p] if off == 0 else mid2[p]
         mine = {**sb, c: one(place[c]), CORE: one(core)}
         for s, sign in enumerate(SIGNS):
-            send(("3far", off), view(got_b, {**sb, c: one(at(c, 2)), CORE: one(cores[s])}), view(hop3[2 * p + s], hop_sb), device(c, sign))
+            far = view(got_b, {**sb, c: one(at(c, 2)), CORE: one(cores[s])})
+            if off == 2:
+                send(("3far", off), far, view(hop4[2 * p + s], {CORE: one(core)}), device(c, sign, 1), 2)
+            else:
+                send(("3far", off), far, view(hop3[2 * p + s], {b: one(off % 4)}), device(c, sign), 2)
         for s, sign in enumerate(SIGNS):
             for k in PAIR:
-                send(("3near", off), view(got_b, {**sb, c: one(at(c, sign)), CORE: one(cores[k])}), view(got[p], mine), device(c, sign, cores[k]))
+                send(("3near", off), view(got_b, {**sb, c: one(at(c, sign)), CORE: one(cores[k])}), view(got[p], mine), device(c, sign, cores[k]), 2)
         send(("3near", off), view(got_b, {**sb, c: one(place[c]), CORE: one(cores[1])}), view(got[p], mine), other, 1)
         got[p][index(mine)] = got_b[index(mine)]
 
     def forward3(p, off):
         a, b, c = ORDERS[p]
         sb = {b: one(at(b, off))}
-        hop_sb = {b: one(off % 4)}
-        for s, sign in enumerate(SIGNS):
-            send(("3fwd", off), view(hop3[2 * p + s], hop_sb), view(got[p], {**sb, c: one(at(c, -sign)), CORE: one(core)}), device(c, sign, cores[s]))
+        for s, sign in enumerate(SIGNS):
+            send(("3fwd", off), view(hop3[2 * p + s], {b: one(off % 4)}), view(got[p], {**sb, c: one(at(c, -sign)), CORE: one(core)}), device(c, sign, cores[s]), 2)
+
+    def last_forward(p, to):
+        a, b, c = ORDERS[p]
+        for s, sign in enumerate(SIGNS):
+            origin = one(1 - to if s else to)
+            send(("3fwd", 2), view(hop4[2 * p + s], {CORE: origin}), view(got[p], {b: one(at(b, 2)), c: one(at(c, -sign)), CORE: origin}), device(c, sign, to), 3)
 
     def length(j):
         return len_buf[4 * me + j]
@@ -338,14 +346,23 @@
     near_units(1)
     far_units(-1)
     last_request([(y, x) for y in OFFSETS[:2] for x in OFFSETS[:2]])
-    arrived(("3far", 2), 3, SIXTEENTH)
-    all_parts(forward3, 2)
+    @pl.when(core == 1)
+    def _():
+        arrived(("3far", 2), 3, EIGHTH)
+        all_parts(last_forward, 0)
+        all_parts(last_forward, 1)
+
     near_units(2)
     far_units(1)
     last_request([(y, x) for y in OFFSETS for x in OFFSETS[:3] if y > 0 or x > 0])
     arrived(("3fwd", 2), 3, SIXTEENTH)
-    taken(send_sem.at[0], 9, {})
+    taken(send_sem.at[0], 6, {})
     taken(send_sem.at[1], 3, EIGHTH)
+    taken(send_sem.at[2], 5, {0: (0, 3), 1: (0, 3)})
+
+    @pl.when(core == 1)
+    def _():
+        taken(send_sem.at[3], 3, EIGHTH)
 
 
 def exchange(c_raw, k_turned, rope_cos, rope_sin, gain, seq_lens, q_lat, q_rope):
@@ -354,7 +371,8 @@
 
     hop1 = [shaped({o[0]: 1, o[1]: 2}) for o in ORDERS for _ in PAIR]
     hop2 = [shaped({o[1]: 1, o[2]: 2}) for o in ORDERS for _ in PAIR]
-    hop3 = [shaped({o[2]: 1, 3: 1}) for o in ORDERS for _ in PAIR]
+    hop3 = [shaped({o[2]: 1, CORE: 1}) for o in ORDERS for _ in PAIR]
+    hop4 = [shaped({o[1]: 1, o[2]: 1}) for o in ORDERS for _ in PAIR]
     small = [
         pltpu.VMEM((8, 64, 512), BF16),
         pltpu.VMEM((8, 32), F32),
@@ -364,7 +382,7 @@
         pltpu.VMEM((4, 16, 512), BF16),
         pltpu.VMEM((4, 16, 64), BF16),
     ]
-    sems = [pltpu.SemaphoreType.DMA((n,)) for n in (LOADS, 2, GROUPS)]
+    sems = [pltpu.SemaphoreType.DMA((n,)) for n in (LOADS, 4, GROUPS)]
     return pl.pallas_call(
         exchange_kernel,
         out_shape=[
@@ -379,7 +397,7 @@
         ],
         in_specs=[pl.BlockSpec(memory_space=pltpu.HBM)] * 8,
         out_specs=[pl.BlockSpec(memory_space=pltpu.VMEM)] * 8,
-        scratch_shapes=[[pltpu.VMEM((9,) + FULL, BF16), shaped({COL: KEY_COLS}), hop1, hop2, hop3, small, sems]],
+        scratch_shapes=[[pltpu.VMEM((9,) + FULL, BF16), shaped({COL: KEY_COLS}), hop1, hop2, hop3, hop4, small, sems]],
         compiler_params=pltpu.CompilerParams(collective_id=0, has_side_effects=True, vmem_limit_bytes=40 * 1024 * 1024),
         name="exchange",
     )(c_raw, k_turned, rope_cos, rope_sin, gain, seq_lens, q_lat, q_rope)

time: 63.3 us -> 63.9 us (level); the launches traced: 62.5 us -> 63.8 us
  Pallas kernels: 61.9 us -> 63.2 us
    pallas_call x1, Pallas kernels: 59.7 us -> 60.9 us  [exchange(): pl.pallas_call(exchange_kernel, out_shape=[pltpu.VMEM((4, 4, 4, 4, 2, 8,...]
where the time goes in v8:
time: 63.9 us; the launch traced here: 63.8 us
  Pallas kernels  63.2 us (99%)
  between operations  0.64 us (1%)
    pallas_call x1, Pallas kernels, exchange(): pl.pallas_call(exchange_kernel, out_shape=[pltpu.VMEM((4, 4, 4, 4, 2, 8,...  60.9 us
    pallas_call x1, Pallas kernels, attend(): pl.pallas_call(attend_kernel, out_shape=[jax.ShapeDtypeStruct(c_cache.sha...  2.21 us

profile of v8, /device:TPU:1, one launch (start us, length us, event | category | flops | bytes accessed | tf_op | source)
XLA Modules:
  0.0 63.8 jit_solution(14059443144671898001)
XLA Ops:
  0.6 60.9 %exchange.1 = (bf16[4,4,4,4,2,8,512]{6,5,4,3,2,1,0:T(8,128)(2,1)S(1)}, bf16[4,64,1024]{2,1,0:T(8,128)(2,1)S(1)}, f32[4,4,4,2,8,128]{5,4,3,2,1,0:T(8,128)S(1)}, s...) custom-call(bf16[4,4,4,2,4,8,512]{6,5,4,3,2,1,0:T(8,128)(2,1)} %bitc, ...), custom_call_target="tpu_custom_call" | custom-call | tf_op jit(solution)/shard_map/exchange/pallas_call | solution.py:386
  61.6 2.2 %attend.1 = (bf16[4,4,4,4,2,8,512]{6,5,4,3,2,1,0:T(8,128)(2,1)}, bf16[4,64,1024]{2,1,0:T(8,128)(2,1)}, bf16[4,16,512]{2,1,0:T(8,128)(2,1)}, bf16[4,4,4,4,2,8,512...) custom-call(bf16[4,4,4,4,2,8,512]{6,5,4,3,2,1,0:T(8,128)(2,1)S(1)} %, ...), custom_call_target="tpu_custom_call", output_to_operand_aliasing={{3}: (0, {}), {4}: (1, {}), {5}: (2, {})} | custom-call | tf_op jit(solution)/shard_map/attend/pallas_call | solution.py:459

commit v9 on v7

--- a/solution.py
+++ b/solution.py
@@ -112,7 +112,8 @@
     me = lax.axis_index("x")
     core = me % 2
     other = me + 1 - 2 * core
-    cores = (core, 1 - core)
+    other_core = 1 - core
+    cores = (core, other_core)
     place = place_of(me)
     at = stepper(place)
 
@@ -216,7 +217,7 @@
         got_b = mid1[p] if off == 0 else mid2[p]
         mine = {**sb, c: one(place[c]), CORE: one(core)}
         for s, sign in enumerate(SIGNS):
-            send(("3far", off), view(got_b, {**sb, c: one(at(c, 2)), CORE: one(cores[s])}), view(hop3[2 * p + s], hop_sb), device(c, sign))
+            send(("3far", off), view(got_b, {**sb, c: one(at(c, 2)), CORE: one(cores[s])}), view(hop3[2 * p + s], hop_sb), device(c, sign, cores[1 - s]))
         for s, sign in enumerate(SIGNS):
             for k in PAIR:
                 send(("3near", off), view(got_b, {**sb, c: one(at(c, sign)), CORE: one(cores[k])}), view(got[p], mine), device(c, sign, cores[k]))
@@ -228,7 +229,7 @@
         sb = {b: one(at(b, off))}
         hop_sb = {b: one(off % 4)}
         for s, sign in enumerate(SIGNS):
-            send(("3fwd", off), view(hop3[2 * p + s], hop_sb), view(got[p], {**sb, c: one(at(c, -sign)), CORE: one(core)}), device(c, sign, cores[s]))
+            send(("3fwd", off), view(hop3[2 * p + s], hop_sb), view(got[p], {**sb, c: one(at(c, -sign)), CORE: one(cores[1 - s])}), device(c, sign, other_core))
 
     def length(j):
         return len_buf[4 * me + j]

time: 63.3 us -> 62.8 us (level); the launches traced: 62.5 us -> 62.7 us
  no operation moved by 1% of the time
where the time goes in v9:
time: 62.8 us; the launch traced here: 62.7 us
  Pallas kernels  62 us (99%)
  between operations  0.64 us (1%)
    pallas_call x1, Pallas kernels, exchange(): pl.pallas_call(exchange_kernel, out_shape=[pltpu.VMEM((4, 4, 4, 4, 2, 8,...  59.8 us
    pallas_call x1, Pallas kernels, attend(): pl.pallas_call(attend_kernel, out_shape=[jax.ShapeDtypeStruct(c_cache.sha...  2.21 us

profile of v9, /device:TPU:1, one launch (start us, length us, event | category | flops | bytes accessed | tf_op | source)
XLA Modules:
  0.0 62.7 jit_solution(15001784614248870615)
XLA Ops:
  0.6 59.8 %exchange.1 = (bf16[4,4,4,4,2,8,512]{6,5,4,3,2,1,0:T(8,128)(2,1)S(1)}, bf16[4,64,1024]{2,1,0:T(8,128)(2,1)S(1)}, f32[4,4,4,2,8,128]{5,4,3,2,1,0:T(8,128)S(1)}, s...) custom-call(bf16[4,4,4,2,4,8,512]{6,5,4,3,2,1,0:T(8,128)(2,1)} %bitc, ...), custom_call_target="tpu_custom_call" | custom-call | tf_op jit(solution)/shard_map/exchange/pallas_call | solution.py:369
  60.5 2.2 %attend.1 = (bf16[4,4,4,4,2,8,512]{6,5,4,3,2,1,0:T(8,128)(2,1)}, bf16[4,64,1024]{2,1,0:T(8,128)(2,1)}, bf16[4,16,512]{2,1,0:T(8,128)(2,1)}, bf16[4,4,4,4,2,8,512...) custom-call(bf16[4,4,4,4,2,8,512]{6,5,4,3,2,1,0:T(8,128)(2,1)S(1)} %, ...), custom_call_target="tpu_custom_call", output_to_operand_aliasing={{3}: (0, {}), {4}: (1, {}), {5}: (2, {})} | custom-call | tf_op jit(solution)/shard_map/attend/pallas_call | solution.py:442

commit v10 on v9

--- a/solution.py
+++ b/solution.py
@@ -19,9 +19,10 @@
 PAIR = range(2)
 REQUESTS = range(4)
 REQ = 512
-GROUPS = 23
-LOADS = 9
+GROUPS = 19
+LOADS = 7
 SIGNS = (1, -1)
+EARLY, LATE = "1fwd and 2far", "2fwd and 3far"
 OFFSETS = (0, -1, 1, 2)
 NT = (((1,), (1,)), ((), ()))
 F32, BF16 = jnp.float32, jnp.bfloat16
@@ -106,7 +107,7 @@
     parts, k_laid, hop1, hop2, hop3, small, sems = scratch
     mid1, mid2 = [[parts.at[3 * stage + p] for p in PARTS] for stage in PAIR]
     got = [got.at[p] for p in PARTS]
-    k_buf, cos_buf, sin_buf, gain_buf, len_buf, qlat_buf, qrope_buf = small
+    k_buf, angles, gain_buf, len_buf, qlat_buf, qrope_buf = small
     load_sem, send_sem, recv_sem = sems
 
     me = lax.axis_index("x")
@@ -151,13 +152,14 @@
         copy.start()
         return copy
 
-    key_loads = [load(i, a, b) for i, (a, b) in enumerate(((k_ref, k_buf), (cos_ref, cos_buf), (sin_ref, sin_buf)))]
-    other_loads = [load(3 + i, a, b) for i, (a, b) in enumerate(((gain_ref, gain_buf), (len_ref, len_buf), (qlat_ref, qlat_buf), (qrope_ref, qrope_buf)))]
+    load(0, cos_ref, angles.at[0])
+    load(0, sin_ref, angles.at[1])
+    small_loads = [load(1 + i, a, b) for i, (a, b) in enumerate(((k_ref, k_buf), (gain_ref, gain_buf), (len_ref, len_buf), (qlat_ref, qlat_buf), (qrope_ref, qrope_buf)))]
     for p in PARTS:
         own = {ORDERS[p][0]: one(place[ORDERS[p][0]])}
-        load(LOADS - 1 if p == 2 else LOADS - 2, taken_from(p, own, False), view(mid1[p], {**own, COL: C_COLS}))
+        load(LOADS - 1, taken_from(p, own, False), view(mid1[p], {**own, COL: C_COLS}))
         if p < 2:
-            load(LOADS - 2, taken_from(p, own, True), view(mid1[p], {**own, COL: K_COLS}))
+            load(LOADS - 1, taken_from(p, own, True), view(mid1[p], {**own, COL: K_COLS}))
 
     slots = {}
 
@@ -174,7 +176,7 @@
         return taken_from(p, sel, True) if p < 2 else view(k_laid, sel)
 
     def first_group(p, cols):
-        return ("1far", cols if p == 2 else None)
+        return ("1far", p == 2 and cols == K_COLS)
 
     def far1(p, cols):
         a, b, _ = ORDERS[p]
@@ -192,14 +194,14 @@
         a, b, _ = ORDERS[p]
         wide = {COL: cols}
         for s, sign in enumerate(SIGNS):
-            send("1fwd", view(hop1[2 * p + s], wide), view(mid1[p], {a: one(at(a, -sign)), b: halves(s), **wide}), device(a, sign))
+            send(EARLY, view(hop1[2 * p + s], wide), view(mid1[p], {a: one(at(a, -sign)), b: halves(s), **wide}), device(a, sign))
 
     def phase2(p, off):
         a, b, c = ORDERS[p]
         sa = {a: one(at(a, off))}
         hop_sa = {a: one(off % 4)}
         for s, sign in enumerate(SIGNS):
-            send(("2far", off), view(mid1[p], {**sa, b: one(at(b, 2)), c: halves(s)}), view(hop2[2 * p + s], hop_sa), device(b, sign))
+            send(EARLY if off == 0 else ("2far", abs(off)), view(mid1[p], {**sa, b: one(at(b, 2)), c: halves(s)}), view(hop2[2 * p + s], hop_sa), device(b, sign))
         for s, sign in enumerate(SIGNS):
             send("2near", view(mid1[p], {**sa, b: one(at(b, sign))}), view(mid2[p], {**sa, b: one(place[b])}), device(b, sign))
 
@@ -208,7 +210,7 @@
         sa = {a: one(at(a, off))}
         hop_sa = {a: one(off % 4)}
         for s, sign in enumerate(SIGNS):
-            send("2fwd", view(hop2[2 * p + s], hop_sa), view(mid2[p], {**sa, b: one(at(b, -sign)), c: halves(s)}), device(b, sign))
+            send(LATE, view(hop2[2 * p + s], hop_sa), view(mid2[p], {**sa, b: one(at(b, -sign)), c: halves(s)}), device(b, sign))
 
     def phase3(p, off):
         a, b, c = ORDERS[p]
@@ -217,7 +219,7 @@
         got_b = mid1[p] if off == 0 else mid2[p]
         mine = {**sb, c: one(place[c]), CORE: one(core)}
         for s, sign in enumerate(SIGNS):
-            send(("3far", off), view(got_b, {**sb, c: one(at(c, 2)), CORE: one(cores[s])}), view(hop3[2 * p + s], hop_sb), device(c, sign, cores[1 - s]))
+            send(LATE if off == -1 else ("3far", off), view(got_b, {**sb, c: one(at(c, 2)), CORE: one(cores[s])}), view(hop3[2 * p + s], hop_sb), device(c, sign, cores[1 - s]))
         for s, sign in enumerate(SIGNS):
             for k in PAIR:
                 send(("3near", off), view(got_b, {**sb, c: one(at(c, sign)), CORE: one(cores[k])}), view(got[p], mine), device(c, sign, cores[k]))
@@ -239,8 +241,8 @@
         diag = row == lax.broadcasted_iota(jnp.int32, (32, 32), 1)
         roped = []
         for pos in range(8):
-            cos = jnp.sum(jnp.where(diag, cos_buf[pos : pos + 1, :], 0.0), axis=1, keepdims=True)
-            sin = jnp.sum(jnp.where(diag, sin_buf[pos : pos + 1, :], 0.0), axis=1, keepdims=True)
+            cos = jnp.sum(jnp.where(diag, angles[0, pos : pos + 1, :], 0.0), axis=1, keepdims=True)
+            sin = jnp.sum(jnp.where(diag, angles[1, pos : pos + 1, :], 0.0), axis=1, keepdims=True)
             lo = k_buf[pos, 0:32, :].astype(F32)
             hi = k_buf[pos, 32:64, :].astype(F32)
             roped.append(jnp.concatenate([lo * cos - hi * sin, hi * cos + lo * sin], axis=0).astype(BF16))
@@ -285,26 +287,25 @@
         all_parts(units, off, OFFSETS[3:])
         key_columns(at(ORDERS[2][1], off))
 
+    BOTH = {0: (0, 3), 2: (0, 2), CORE: one(0)}
     EIGHTH, SIXTEENTH = {0: one(0), 1: (0, 2)}, {0: one(0), 1: one(0)}
     pl.semaphore_wait(barrier, 13)
     for first in (far1, near1):
         all_parts(first, C_COLS)
         first(0, K_COLS)
         first(1, K_COLS)
-    for copy in key_loads:
-        copy.wait()
+    pltpu.make_async_copy(angles, angles, load_sem.at[0]).wait()
+    small_loads[0].wait()
     keys()
-    for copy in other_loads:
+    for copy in small_loads[1:]:
         copy.wait()
     queries()
     far1(2, K_COLS)
     near1(2, K_COLS)
-    taken(load_sem.at[LOADS - 2], 2, {0: one(0)})
-    taken(load_sem.at[LOADS - 1], 1, {0: one(0), COL: C_COLS})
-    arrived(first_group(0, None), 2, {0: one(0)})
+    taken(load_sem.at[LOADS - 1], 4, {0: one(0), COL: C_COLS})
+    arrived(first_group(2, C_COLS), 4, {0: one(0), COL: C_COLS})
     forward1(0)
     forward1(1)
-    arrived(first_group(2, C_COLS), 1, {0: one(0), COL: C_COLS})
     forward1(2, C_COLS)
     all_parts(phase2, 0)
     arrived(first_group(2, K_COLS), 1, {0: one(0), COL: K_COLS})
@@ -312,13 +313,12 @@
     arrived("1near", 3, {0: (0, 2)})
     all_parts(phase2, -1)
     all_parts(phase2, 1)
-    arrived(("2far", 0), 3, SIXTEENTH)
+    arrived(EARLY, 5, BOTH)
     all_parts(forward2, 0)
-    arrived("1fwd", 3, {0: one(0)})
     all_parts(phase2, 2)
-    for off in (-1, 1):
-        arrived(("2far", off), 3, SIXTEENTH)
-        all_parts(forward2, off)
+    arrived(("2far", 1), 3, {0: one(0), 1: (0, 2)})
+    all_parts(forward2, -1)
+    all_parts(forward2, 1)
     arrived(("2far", 2), 3, SIXTEENTH)
     all_parts(forward2, 2)
     all_parts(phase3, 0)
@@ -328,8 +328,7 @@
     all_parts(forward3, 0)
     all_parts(phase3, 1)
     near_units(0)
-    arrived("2fwd", 3, {0: one(0)})
-    arrived(("3far", -1), 3, SIXTEENTH)
+    arrived(LATE, 5, BOTH)
     all_parts(forward3, -1)
     all_parts(phase3, 2)
     near_units(-1)
@@ -338,12 +337,12 @@
     all_parts(forward3, 1)
     near_units(1)
     far_units(-1)
-    last_request([(y, x) for y in OFFSETS[:2] for x in OFFSETS[:2]])
+    last_request([(y, x) for y in OFFSETS[:3] for x in OFFSETS[:2]])
     arrived(("3far", 2), 3, SIXTEENTH)
     all_parts(forward3, 2)
     near_units(2)
     far_units(1)
-    last_request([(y, x) for y in OFFSETS for x in OFFSETS[:3] if y > 0 or x > 0])
+    last_request([(2, x) for x in OFFSETS[:2]] + [(y, 1) for y in OFFSETS])
     arrived(("3fwd", 2), 3, SIXTEENTH)
     taken(send_sem.at[0], 9, {})
     taken(send_sem.at[1], 3, EIGHTH)
@@ -358,8 +357,7 @@
     hop3 = [shaped({o[2]: 1, 3: 1}) for o in ORDERS for _ in PAIR]
     small = [
         pltpu.VMEM((8, 64, 512), BF16),
-        pltpu.VMEM((8, 32), F32),
-        pltpu.VMEM((8, 32), F32),
+        pltpu.VMEM((2, 8, 32), F32),
         pltpu.VMEM((LATENT,), BF16),
         pltpu.SMEM((REQ,), jnp.int32),
         pltpu.VMEM((4, 16, 512), BF16),

time: 62.8 us -> 62.7 us (level)
  no operation moved by 1% of the time
where the time goes in v10:
time: 62.7 us; the launch traced here: 62.6 us
  Pallas kernels  62 us (99%)
  between operations  0.64 us (1%)
    pallas_call x1, Pallas kernels, exchange(): pl.pallas_call(exchange_kernel, out_shape=[pltpu.VMEM((4, 4, 4, 4, 2, 8,...  59.8 us
    pallas_call x1, Pallas kernels, attend(): pl.pallas_call(attend_kernel, out_shape=[jax.ShapeDtypeStruct(c_cache.sha...  2.21 us

profile of v10, /device:TPU:1, one launch (start us, length us, event | category | flops | bytes accessed | tf_op | source)
XLA Modules:
  0.0 62.6 jit_solution(4684281138228304375)
XLA Ops:
  0.6 59.8 %exchange.1 = (bf16[4,4,4,4,2,8,512]{6,5,4,3,2,1,0:T(8,128)(2,1)S(1)}, bf16[4,64,1024]{2,1,0:T(8,128)(2,1)S(1)}, f32[4,4,4,2,8,128]{5,4,3,2,1,0:T(8,128)S(1)}, s...) custom-call(bf16[4,4,4,2,4,8,512]{6,5,4,3,2,1,0:T(8,128)(2,1)} %bitc, ...), custom_call_target="tpu_custom_call" | custom-call | tf_op jit(solution)/shard_map/exchange/pallas_call | solution.py:367
  60.4 2.2 %attend.1 = (bf16[4,4,4,4,2,8,512]{6,5,4,3,2,1,0:T(8,128)(2,1)}, bf16[4,64,1024]{2,1,0:T(8,128)(2,1)}, bf16[4,16,512]{2,1,0:T(8,128)(2,1)}, bf16[4,4,4,4,2,8,512...) custom-call(bf16[4,4,4,4,2,8,512]{6,5,4,3,2,1,0:T(8,128)(2,1)S(1)} %, ...), custom_call_target="tpu_custom_call", output_to_operand_aliasing={{3}: (0, {}), {4}: (1, {}), {5}: (2, {})} | custom-call | tf_op jit(solution)/shard_map/attend/pallas_call | solution.py:440

commit v11 on v10

--- a/solution.py
+++ b/solution.py
@@ -390,7 +390,7 @@
 
     def write(a, b):
         writes.append(pltpu.make_async_copy(a, b, sem))
-        writes[-1].start()
+        writes[-1].start(priority=len(writes) % 2)
 
     def write_rows(j, sel):
         where = (j,) + index(sel)

time: 62.7 us -> 62.7 us (level)
  no operation moved by 1% of the time
where the time goes in v11:
time: 62.7 us; the launch traced here: 62.6 us
  Pallas kernels  62 us (99%)
  between operations  0.64 us (1%)
    pallas_call x1, Pallas kernels, exchange(): pl.pallas_call(exchange_kernel, out_shape=[pltpu.VMEM((4, 4, 4, 4, 2, 8,...  59.8 us
    pallas_call x1, Pallas kernels, attend(): pl.pallas_call(attend_kernel, out_shape=[jax.ShapeDtypeStruct(c_cache.sha...  2.21 us

profile of v11, /device:TPU:1, one launch (start us, length us, event | category | flops | bytes accessed | tf_op | source)
XLA Modules:
  0.0 62.6 jit_solution(10585648701640480483)
XLA Ops:
  0.6 59.8 %exchange.1 = (bf16[4,4,4,4,2,8,512]{6,5,4,3,2,1,0:T(8,128)(2,1)S(1)}, bf16[4,64,1024]{2,1,0:T(8,128)(2,1)S(1)}, f32[4,4,4,2,8,128]{5,4,3,2,1,0:T(8,128)S(1)}, s...) custom-call(bf16[4,4,4,2,4,8,512]{6,5,4,3,2,1,0:T(8,128)(2,1)} %bitc, ...), custom_call_target="tpu_custom_call" | custom-call | tf_op jit(solution)/shard_map/exchange/pallas_call | solution.py:367
  60.4 2.2 %attend.1 = (bf16[4,4,4,4,2,8,512]{6,5,4,3,2,1,0:T(8,128)(2,1)}, bf16[4,64,1024]{2,1,0:T(8,128)(2,1)}, bf16[4,16,512]{2,1,0:T(8,128)(2,1)}, bf16[4,4,4,4,2,8,512...) custom-call(bf16[4,4,4,4,2,8,512]{6,5,4,3,2,1,0:T(8,128)(2,1)S(1)} %, ...), custom_call_target="tpu_custom_call", output_to_operand_aliasing={{3}: (0, {}), {4}: (1, {}), {5}: (2, {})} | custom-call | tf_op jit(solution)/shard_map/attend/pallas_call | solution.py:440

commit v12 on v11

--- a/solution.py
+++ b/solution.py
@@ -417,8 +417,6 @@
     for p, (_, b, c) in enumerate(ORDERS):
         write_rows(p, {b: one(at(b, far)), c: one(at(c, far))})
     write_rows(3, {2: one(at(2, far))})
-    key_columns(at(ORDERS[2][1], far))
-    write_keys(at(ORDERS[2][1], far))
 
     row = lax.broadcasted_iota(jnp.int32, (POSITIONS, LANES), 0)
     masked = jnp.where(row < len_ref[4, 0:1, :], scores[...].reshape(POSITIONS, LANES) * ATTN_SCALE, -1e30)
@@ -430,6 +428,9 @@
         weighted = jnp.dot(rounded[mine], c_buf[j].reshape(POSITIONS, LATENT), preferred_element_type=F32)
         o_buf[j] = (weighted / weight_sum[mine]).astype(BF16)
         write(o_buf.at[j], o_hbm.at[j])
+        if j == 2:
+            key_columns(at(ORDERS[2][1], far))
+            write_keys(at(ORDERS[2][1], far))
     for copy in writes:
         copy.wait()
 

time: 62.7 us -> 62.8 us (level)
  no operation moved by 1% of the time
where the time goes in v12:
time: 62.8 us; the launch traced here: 62.7 us
  Pallas kernels  62.1 us (99%)
  between operations  0.64 us (1%)
    pallas_call x1, Pallas kernels, exchange(): pl.pallas_call(exchange_kernel, out_shape=[pltpu.VMEM((4, 4, 4, 4, 2, 8,...  59.8 us
    pallas_call x1, Pallas kernels, attend(): pl.pallas_call(attend_kernel, out_shape=[jax.ShapeDtypeStruct(c_cache.sha...  2.28 us

profile of v12, /device:TPU:1, one launch (start us, length us, event | category | flops | bytes accessed | tf_op | source)
XLA Modules:
  0.0 62.7 jit_solution(12876438237657691852)
XLA Ops:
  0.6 59.8 %exchange.1 = (bf16[4,4,4,4,2,8,512]{6,5,4,3,2,1,0:T(8,128)(2,1)S(1)}, bf16[4,64,1024]{2,1,0:T(8,128)(2,1)S(1)}, f32[4,4,4,2,8,128]{5,4,3,2,1,0:T(8,128)S(1)}, s...) custom-call(bf16[4,4,4,2,4,8,512]{6,5,4,3,2,1,0:T(8,128)(2,1)} %bitc, ...), custom_call_target="tpu_custom_call" | custom-call | tf_op jit(solution)/shard_map/exchange/pallas_call | solution.py:367
  60.4 2.3 %attend.1 = (bf16[4,4,4,4,2,8,512]{6,5,4,3,2,1,0:T(8,128)(2,1)}, bf16[4,64,1024]{2,1,0:T(8,128)(2,1)}, bf16[4,16,512]{2,1,0:T(8,128)(2,1)}, bf16[4,4,4,4,2,8,512...) custom-call(bf16[4,4,4,4,2,8,512]{6,5,4,3,2,1,0:T(8,128)(2,1)S(1)} %, ...), custom_call_target="tpu_custom_call", output_to_operand_aliasing={{3}: (0, {}), {4}: (1, {}), {5}: (2, {})} | custom-call | tf_op jit(solution)/shard_map/attend/pallas_call | solution.py:441

commit v13 on v11

--- a/solution.py
+++ b/solution.py
@@ -412,13 +412,13 @@
 
     got = [got_ref.at[p] for p in PARTS]
     units, last_request, key_columns = row_work(at, lambda j: len_ref[j, 0:1, 0:1], got, lambda: gain_ref[0:1, :], q_cols, qk_cols, c_buf, kr_buf, scores)
+    key_columns(at(ORDERS[2][1], far))
+    write_keys(at(ORDERS[2][1], far))
     all_parts(units, far, OFFSETS[3:])
     last_request([(y, far) for y in OFFSETS])
     for p, (_, b, c) in enumerate(ORDERS):
         write_rows(p, {b: one(at(b, far)), c: one(at(c, far))})
     write_rows(3, {2: one(at(2, far))})
-    key_columns(at(ORDERS[2][1], far))
-    write_keys(at(ORDERS[2][1], far))
 
     row = lax.broadcasted_iota(jnp.int32, (POSITIONS, LANES), 0)
     masked = jnp.where(row < len_ref[4, 0:1, :], scores[...].reshape(POSITIONS, LANES) * ATTN_SCALE, -1e30)

time: 62.7 us -> 62.7 us (level)
  no operation moved by 1% of the time
where the time goes in v13:
time: 62.7 us; the launch traced here: 62.6 us
  Pallas kernels  62 us (99%)
  between operations  0.64 us (1%)
    pallas_call x1, Pallas kernels, exchange(): pl.pallas_call(exchange_kernel, out_shape=[pltpu.VMEM((4, 4, 4, 4, 2, 8,...  59.8 us
    pallas_call x1, Pallas kernels, attend(): pl.pallas_call(attend_kernel, out_shape=[jax.ShapeDtypeStruct(c_cache.sha...  2.22 us

profile of v13, /device:TPU:1, one launch (start us, length us, event | category | flops | bytes accessed | tf_op | source)
XLA Modules:
  0.0 62.6 jit_solution(11094049261389808186)
XLA Ops:
  0.6 59.8 %exchange.1 = (bf16[4,4,4,4,2,8,512]{6,5,4,3,2,1,0:T(8,128)(2,1)S(1)}, bf16[4,64,1024]{2,1,0:T(8,128)(2,1)S(1)}, f32[4,4,4,2,8,128]{5,4,3,2,1,0:T(8,128)S(1)}, s...) custom-call(bf16[4,4,4,2,4,8,512]{6,5,4,3,2,1,0:T(8,128)(2,1)} %bitc, ...), custom_call_target="tpu_custom_call" | custom-call | tf_op jit(solution)/shard_map/exchange/pallas_call | solution.py:367
  60.4 2.2 %attend.1 = (bf16[4,4,4,4,2,8,512]{6,5,4,3,2,1,0:T(8,128)(2,1)}, bf16[4,64,1024]{2,1,0:T(8,128)(2,1)}, bf16[4,16,512]{2,1,0:T(8,128)(2,1)}, bf16[4,4,4,4,2,8,512...) custom-call(bf16[4,4,4,4,2,8,512]{6,5,4,3,2,1,0:T(8,128)(2,1)S(1)} %, ...), custom_call_target="tpu_custom_call", output_to_operand_aliasing={{3}: (0, {}), {4}: (1, {}), {5}: (2, {})} | custom-call | tf_op jit(solution)/shard_map/attend/pallas_call | solution.py:440

commit v14 on v10

--- a/solution.py
+++ b/solution.py
@@ -406,13 +406,13 @@
             write_rows(p, {b: one(at(b, off))})
         for off in near:
             write_rows(p, {b: one(at(b, far)), c: one(at(c, off))})
+
+    got = [got_ref.at[p] for p in PARTS]
+    units, last_request, key_columns = row_work(at, lambda j: len_ref[j, 0:1, 0:1], got, lambda: gain_ref[0:1, :], q_cols, qk_cols, c_buf, kr_buf, scores)
+    all_parts(units, far, OFFSETS[3:])
     for off in near:
         write_rows(3, {2: one(at(2, off))})
         write_keys(at(ORDERS[2][1], off))
-
-    got = [got_ref.at[p] for p in PARTS]
-    units, last_request, key_columns = row_work(at, lambda j: len_ref[j, 0:1, 0:1], got, lambda: gain_ref[0:1, :], q_cols, qk_cols, c_buf, kr_buf, scores)
-    all_parts(units, far, OFFSETS[3:])
     last_request([(y, far) for y in OFFSETS])
     for p, (_, b, c) in enumerate(ORDERS):
         write_rows(p, {b: one(at(b, far)), c: one(at(c, far))})

time: 62.7 us -> 62.8 us (level)
  no operation moved by 1% of the time
where the time goes in v14:
time: 62.8 us; the launch traced here: 62.7 us
  Pallas kernels  62 us (99%)
  between operations  0.64 us (1%)
    pallas_call x1, Pallas kernels, exchange(): pl.pallas_call(exchange_kernel, out_shape=[pltpu.VMEM((4, 4, 4, 4, 2, 8,...  59.8 us
    pallas_call x1, Pallas kernels, attend(): pl.pallas_call(attend_kernel, out_shape=[jax.ShapeDtypeStruct(c_cache.sha...  2.27 us

profile of v14, /device:TPU:1, one launch (start us, length us, event | category | flops | bytes accessed | tf_op | source)
XLA Modules:
  0.0 62.7 jit_solution(5158399985430476123)
XLA Ops:
  0.6 59.8 %exchange.1 = (bf16[4,4,4,4,2,8,512]{6,5,4,3,2,1,0:T(8,128)(2,1)S(1)}, bf16[4,64,1024]{2,1,0:T(8,128)(2,1)S(1)}, f32[4,4,4,2,8,128]{5,4,3,2,1,0:T(8,128)S(1)}, s...) custom-call(bf16[4,4,4,2,4,8,512]{6,5,4,3,2,1,0:T(8,128)(2,1)} %bitc, ...), custom_call_target="tpu_custom_call" | custom-call | tf_op jit(solution)/shard_map/exchange/pallas_call | solution.py:367
  60.4 2.3 %attend.1 = (bf16[4,4,4,4,2,8,512]{6,5,4,3,2,1,0:T(8,128)(2,1)}, bf16[4,64,1024]{2,1,0:T(8,128)(2,1)}, bf16[4,16,512]{2,1,0:T(8,128)(2,1)}, bf16[4,4,4,4,2,8,512...) custom-call(bf16[4,4,4,4,2,8,512]{6,5,4,3,2,1,0:T(8,128)(2,1)S(1)} %, ...), custom_call_target="tpu_custom_call", output_to_operand_aliasing={{3}: (0, {}), {4}: (1, {}), {5}: (2, {})} | custom-call | tf_op jit(solution)/shard_map/attend/pallas_call | solution.py:440
